TPU v7x, 512 devices: a whole 4x8x8 slice. The times are simulated.
512 devices in a mesh: slab: 128 (over y, z, core), cross: 4 (over x).
Axes of the slice: x: 4, y: 8, z: 8, core: 2. Of those that a mesh axis runs over, the one named last changes fastest.
Arguments:
- a_tiles: bfloat16 [1024, 7, 128, 128], P(('slab', 'cross')), may hold values from -0.1875 to 0.1875
- a_cols: int32 [1024, 7], P(('slab', 'cross')), may hold values from 0 to 17, as said below
- over_tiles: bfloat16 [2048, 128, 128], P(('slab', 'cross')), may hold values from -0.1875 to 0.1875
- over_rows: int32 [2048], P(('slab', 'cross')), may hold values from 0 to 1
- over_cols: int32 [2048], P(('slab', 'cross')), may hold values from 0 to 17
- p_tiles: bfloat16 [1024, 3, 128, 128], P(('slab', 'cross')), may hold values from -0.8984375 to 0.8984375
- p_cols: int32 [1024, 3], P(('slab', 'cross')), may hold values from 0 to 5, as said below
Outputs:
- coarse: float32 [32768, 1792], P(('slab', 'cross'))
Inputs may be any that keep to these rules, and one draw needn't show every extreme that they name: `a_cols`: the 7 entries of a row are different. `p_cols`: the 3 entries of a row are different.
All inputs are finite; a program needn't handle non-finite values.
Results may differ from a plain program's by a relative error of at most 0.0063.
Values may be sent and summed in bfloat16 or wider, within the bound.
A program may use at most 64 MiB of HBM per device.

v0:
```python
import jax
import jax.numpy as jnp
from jax import lax
from jax.sharding import PartitionSpec as P

CB = 2


def with_halo(block, sides, width):
    for axis, dim in sides:
        count = lax.axis_size(axis)
        forward = [(i, i + 1) for i in range(count - 1)]
        backward = [(target, source) for source, target in forward]
        low = lax.ppermute(
            lax.slice_in_dim(block, block.shape[dim] - width, None, axis=dim), axis, forward
        )
        high = lax.ppermute(lax.slice_in_dim(block, 0, width, axis=dim), axis, backward)
        block = jnp.concatenate([low, block, high], axis=dim)
    return block


def from_behind(value, axis, by):
    devices = lax.axis_size(axis)
    pairs = [(i, i + by) for i in range(devices) if 0 <= i + by < devices]
    return lax.ppermute(value, axis, pairs)


def split_up(value, dim, devices):
    dims = value.shape
    blocks = value.reshape(*dims[:dim], devices, dims[dim] // devices, *dims[dim + 1 :])
    return jnp.moveaxis(blocks, dim, 0)


def sent_and_summed(value, axis, dim):
    devices = lax.axis_size(axis)
    blocks = lax.all_to_all(split_up(value, dim, devices), axis, 0, 0, tiled=True)
    return jnp.sum(blocks.astype(jnp.float32), axis=0)


def place_rows(lower, middle, upper, width):
    total = jnp.zeros((middle.shape[0], 7 * width), jnp.float32)
    total = total.at[:, 0 : 5 * width].add(lower)
    total = total.at[:, width : 6 * width].add(middle)
    total = total.at[:, 2 * width : 7 * width].add(upper)
    return total


def body(a_tiles, a_cols, over_tiles, over_rows, over_cols, p_tiles, p_cols):
    blocks = a_tiles.shape[0]
    tile_size = a_tiles.shape[-1]
    width = CB * tile_size
    wide = 3 * width
    span = blocks * tile_size
    p_picks = (p_cols[:, :, None] == jnp.arange(3 * CB, dtype=jnp.int32)[None, None, :]).astype(
        jnp.bfloat16
    )
    dense_p = jnp.einsum("nmq,nmab->naqb", p_picks, p_tiles, preferred_element_type=jnp.float32)
    dense_p = dense_p.astype(jnp.bfloat16).reshape(span, wide)
    got_tiles, got_picks = (
        with_halo(p_tiles.reshape((1, 1) + p_tiles.shape), (("slab", 0), ("cross", 1)), 1),
        with_halo(p_picks.reshape((1, 1) + p_picks.shape), (("slab", 0), ("cross", 1)), 1),
    )
    extended = jnp.einsum(
        "xynmq,xynmab->xynaqb", got_picks, got_tiles, preferred_element_type=jnp.float32
    )
    extended = extended.astype(jnp.bfloat16).reshape(9 * blocks, tile_size, wide)
    product = jnp.zeros((blocks, tile_size, 5 * width), jnp.float32)
    for k_index in range(a_cols.shape[1]):
        rows = jnp.take(extended, a_cols[:, k_index], axis=0)
        piece = jnp.einsum(
            "nab,nbq->naq", a_tiles[:, k_index], rows, preferred_element_type=jnp.float32
        )
        offsets = a_cols[:, k_index] // (3 * blocks)
        for shift_index in range(3):
            mask = (offsets == shift_index).astype(jnp.float32)[:, None, None]
            product = product.at[:, :, shift_index * width : shift_index * width + wide].add(
                mask * piece
            )
    rows = jnp.take(extended, over_cols, axis=0)
    piece = jnp.einsum("oab,obq->oaq", over_tiles, rows, preferred_element_type=jnp.float32)
    row_pick = (over_rows[:, None] == jnp.arange(blocks, dtype=jnp.int32)[None, :]).astype(
        jnp.float32
    )
    offsets = over_cols // (3 * blocks)
    for shift_index in range(3):
        select = row_pick * (offsets == shift_index).astype(jnp.float32)[:, None]
        contrib = jnp.einsum("on,oaq->naq", select, piece)
        product = product.at[:, :, shift_index * width : shift_index * width + wide].add(contrib)
    product = product.astype(jnp.bfloat16).reshape(span, 5 * width)
    partial_value = lax.dot_general(
        dense_p, product, (((0,), (0,)), ((), ())), preferred_element_type=jnp.float32
    )
    partial_value = partial_value.reshape(3, width, 5 * width)
    upper = from_behind(partial_value[0].astype(jnp.bfloat16), "slab", -1).astype(jnp.float32)
    lower = from_behind(partial_value[2].astype(jnp.bfloat16), "slab", 1).astype(jnp.float32)
    owned = place_rows(lower, partial_value[1], upper, width)
    return sent_and_summed(owned.astype(jnp.bfloat16), "cross", 0)


def solution(mesh):
    return jax.shard_map(
        body,
        mesh=mesh,
        in_specs=(
            P(("slab", "cross"), None, None, None),
            P(("slab", "cross"), None),
            P(("slab", "cross"), None, None),
            P(("slab", "cross")),
            P(("slab", "cross")),
            P(("slab", "cross"), None, None, None),
            P(("slab", "cross"), None),
        ),
        out_specs=P(("slab", "cross"), None),
        check_vma=False,
    )
```

profile of v0, /device:TPU:56, one launch (start us, length us, event | category | flops | bytes accessed | tf_op | source)
XLA Modules:
  0.0 128.0 jit_solution(988439212029307377)
XLA Ops:
  0.0 1.1 copy.110
  1.1 1.9 %collective-permute-start = (bf16[1,1,2,3,128,128]{5,3,4,2,1,0:T(4,128)(2,1)S(1)}, bf16[1,1,2,3,128,128]{5,3,4,2,1,0:T(4,128)(2,1)S(1)}, u32[]{:S(2)}, u32[]{:S(2)}) collective-permute-start(bf16[1,1,2,3,128,128]{5,3,4,2,1,0:T(4,128)(2,1)S(1)} %bitcast.144), channel_id=1, source_target_pairs={{0,4},{4,8},{8,12},{12,16},{16,20},{20,24},{24,28},{28,32},{32,36}... | collective-permute-start | bytes 589832 | tf_op jit(solution)/shard_map/ppermute | solution.py:14
  3.1 11.2 %collective-permute-start.1 = (bf16[1,1,2,3,128,128]{5,3,4,2,1,0:T(4,128)(2,1)S(1)}, bf16[1,1,2,3,128,128]{5,3,4,2,1,0:T(4,128)(2,1)S(1)}, u32[]{:S(2)}, u32[]{:S(2)}) collective-permute-start(bf16[1,1,2,3,128,128]{5,3,4,2,1,0:T(4,128)(2,1)S(1)} %bitcast.145), channel_id=1, source_target_pairs={{4,0},{8,4},{12,8},{16,12},{20,16},{24,20},{28,24},{32,28},{36,32}... | collective-permute-start | bytes 589832 | tf_op jit(solution)/shard_map/ppermute | solution.py:17
  14.2 0.8 fusion.93
  15.0 1.9 %collective-permute-start.4 = (bf16[1,1,2,3,6]{4,3,2,1,0:T(4,128)(2,1)S(1)}, bf16[1,1,2,3,6]{4,3,2,1,0:T(4,128)(2,1)S(1)}, u32[]{:S(2)}, u32[]{:S(2)}) collective-permute-start(bf16[1,1,2,3,6]{4,3,2,1,0:T(4,128)(2,1)S(1)} %fusion.93), channel_id=1, source_target_pairs={{0,4},{4,8},{8,12},{12,16},{16,20},{20,24},{24,28},{28,32},{32,36}... | collective-permute-start | bytes 224 | tf_op jit(solution)/shard_map/ppermute | solution.py:14
  16.9 5.8 %collective-permute-start.5 = (bf16[1,1,2,3,6]{4,3,2,1,0:T(4,128)(2,1)S(1)}, bf16[1,1,2,3,6]{4,3,2,1,0:T(4,128)(2,1)S(1)}, u32[]{:S(2)}, u32[]{:S(2)}) collective-permute-start(bf16[1,1,2,3,6]{4,3,2,1,0:T(4,128)(2,1)S(1)} %fusion.93), channel_id=1, source_target_pairs={{4,0},{8,4},{12,8},{16,12},{20,16},{24,20},{28,24},{32,28},{36,32}... | collective-permute-start | bytes 224 | tf_op jit(solution)/shard_map/ppermute | solution.py:17
  22.7 1.2 slice_reduce_fusion
  24.2 0.7 compare_convert_fusion
  24.9 0.7 compare_select_fusion.7
  25.6 0.7 pad_maximum_fusion
  26.4 3.4 %collective-permute-start.2 = (bf16[3,1,2,3,128,128]{5,4,3,2,1,0:T(8,128)(2,1)S(1)}, bf16[3,1,2,3,128,128]{5,4,3,2,1,0:T(8,128)(2,1)S(1)}, u32[]{:S(2)}, u32[]{:S(2)}) collective-permute-start(bf16[3,1,2,3,128,128]{5,4,3,2,1,0:T(8,128)(2,1)S(1)} %copy.52), channel_id=1, source_target_pairs={{0,1},{1,2},{2,3},{4,5},{5,6},{6,7},{8,9},{9,10},{10,11},{12,13},{... | collective-permute-start | bytes 1769480 | tf_op jit(solution)/shard_map/ppermute | solution.py:14
  29.8 1.3 %collective-permute-start.3 = (bf16[3,1,2,3,128,128]{5,4,3,2,1,0:T(8,128)(2,1)S(1)}, bf16[3,1,2,3,128,128]{5,4,3,2,1,0:T(8,128)(2,1)S(1)}, u32[]{:S(2)}, u32[]{:S(2)}) collective-permute-start(bf16[3,1,2,3,128,128]{5,4,3,2,1,0:T(8,128)(2,1)S(1)} %copy.52), channel_id=1, source_target_pairs={{1,0},{2,1},{3,2},{5,4},{6,5},{7,6},{9,8},{10,9},{11,10},{13,12},{... | collective-permute-start | bytes 1769480 | tf_op jit(solution)/shard_map/ppermute | solution.py:17
  31.7 4.5 %collective-permute-start.6 = (bf16[3,1,2,3,6]{4,3,2,1,0:T(4,128)(2,1)S(1)}, bf16[3,1,2,3,6]{4,3,2,1,0:T(4,128)(2,1)S(1)}, u32[]{:S(2)}, u32[]{:S(2)}) collective-permute-start(bf16[3,1,2,3,6]{4,3,2,1,0:T(4,128)(2,1)S(1)} %pad_maximum_fusion.1), channel_id=1, source_target_pairs={{0,1},{1,2},{2,3},{4,5},{5,6},{6,7},{8,9},{9,10},{10,11},{12,13},{... | collective-permute-start | bytes 656 | tf_op jit(solution)/shard_map/ppermute | solution.py:14
  36.2 1.5 %collective-permute-start.7 = (bf16[3,1,2,3,6]{4,3,2,1,0:T(4,128)(2,1)S(1)}, bf16[3,1,2,3,6]{4,3,2,1,0:T(4,128)(2,1)S(1)}, u32[]{:S(2)}, u32[]{:S(2)}) collective-permute-start(bf16[3,1,2,3,6]{4,3,2,1,0:T(4,128)(2,1)S(1)} %pad_maximum_fusion.1), channel_id=1, source_target_pairs={{1,0},{2,1},{3,2},{5,4},{6,5},{7,6},{9,8},{10,9},{11,10},{13,12},{... | collective-permute-start | bytes 656 | tf_op jit(solution)/shard_map/ppermute | solution.py:17
  37.7 1.5 %collective-permute-done.2 = bf16[3,1,2,3,128,128]{5,4,3,2,1,0:T(8,128)(2,1)S(1)} collective-permute-done((bf16[3,1,2,3,128,128]{5,4,3,2,1,0:T(8,128)(2,1)S(1)}, bf16[3,1,2,3,128,128]{5,4,3,2,1,0:T(8,128)(2,1)S(1)}, u32[]{:S(2)}, u32[]{:S(2)}) %collective-permute-start.2) | collective-permute-done | bytes 589856 | tf_op jit(solution)/shard_map/ppermute | solution.py:14
  39.2 0.5 copy.54
  39.7 3.6 %collective-permute-done.3 = bf16[3,1,2,3,128,128]{5,4,3,2,1,0:T(8,128)(2,1)S(1)} collective-permute-done((bf16[3,1,2,3,128,128]{5,4,3,2,1,0:T(8,128)(2,1)S(1)}, bf16[3,1,2,3,128,128]{5,4,3,2,1,0:T(8,128)(2,1)S(1)}, u32[]{:S(2)}, u32[]{:S(2)}) %collective-permute-start.3) | collective-permute-done | bytes 589856 | tf_op jit(solution)/shard_map/ppermute | solution.py:17
  43.4 0.5 copy.55
  43.9 3.1 %convert_bitcast_fusion = bf16[3,3,2,128,6,128]{5,4,3,2,1,0:T(8,128)(2,1)} fusion(bf16[3,1,2,3,128,128]{5,3,4,2,1,0:T(4,128)(2,1)S(1)} %copy.55, bf16[1,1,2,3,128,128]{5,3,4,2,1,0:T(4,128)(2,1)S(1)} %collective-permute-done.1, bf16[1,1,2,3,128,128]{5,3,4,2,1,0:T(4,128)(2,1)S(1)} %bitcast.147, bf16[1,1,2,3,128,128]{5,3,4,2,1,0:T(4,128)(2,1)S(1)} %collective-permute-done, ...), kind=kOutput, calls=%fused_computation.8 | convolution fusion | flops 21236904 | bytes 5309064 | tf_op jit(solution)/shard_map/xynmq,xynmab->xynaqb/dot_general | solution.py:63
  47.1 6.6 %copy.56 = bf16[3,3,2,128,6,128]{3,5,4,2,1,0:T(8,128)(2,1)} copy(bf16[3,3,2,128,6,128]{5,4,3,2,1,0:T(8,128)(2,1)} %convert_bitcast_fusion) | data formatting | bytes 7077888 | tf_op jit(solution)/shard_map/convert_element_type | solution.py:66
  53.7 5.8 %copy.71 = bf16[18,128,768]{2,1,0:T(8,128)(2,1)} copy(bf16[18,128,768]{1,2,0:T(8,128)(2,1)} %bitcast.133) | data formatting | bytes 7077888 | tf_op jit(solution)/shard_map/reshape | solution.py:66
  59.4 3.3 %gather_fusion.1 = bf16[2,128,768]{1,2,0:T(8,128)(2,1)} fusion(bf16[18,128,768]{1,2,0:T(8,128)(2,1)} %bitcast.134, s32[1024]{0:T(1024)S(1)} %pad_clamp_fusion.7), kind=kCustom, calls=%fused_computation.clone | custom fusion | bytes 786440 | tf_op jit(solution)/shard_map/jit(_take)/gather | solution.py:69
  62.8 3.4 %gather_fusion.2 = bf16[2,128,768]{1,2,0:T(8,128)(2,1)} fusion(bf16[18,128,768]{1,2,0:T(8,128)(2,1)} %bitcast.135, s32[1024]{0:T(1024)S(1)} %pad_clamp_fusion.6), kind=kCustom, calls=%fused_computation.1.clone | custom fusion | bytes 786440 | tf_op jit(solution)/shard_map/jit(_take)/gather | solution.py:69
  66.1 3.4 %gather_fusion.3 = bf16[2,128,768]{1,2,0:T(8,128)(2,1)} fusion(bf16[18,128,768]{1,2,0:T(8,128)(2,1)} %bitcast.136, s32[1024]{0:T(1024)S(1)} %pad_clamp_fusion.5), kind=kCustom, calls=%fused_computation.2.clone | custom fusion | bytes 786440 | tf_op jit(solution)/shard_map/jit(_take)/gather | solution.py:69
  69.5 3.4 %gather_fusion.4 = bf16[2,128,768]{1,2,0:T(8,128)(2,1)} fusion(bf16[18,128,768]{1,2,0:T(8,128)(2,1)} %bitcast.137, s32[1024]{0:T(1024)S(1)} %pad_clamp_fusion.4), kind=kCustom, calls=%fused_computation.3.clone | custom fusion | bytes 786440 | tf_op jit(solution)/shard_map/jit(_take)/gather | solution.py:69
  72.8 2.6 %gather_fusion.5 = bf16[2,128,768]{1,2,0:T(8,128)(2,1)S(1)} fusion(bf16[18,128,768]{1,2,0:T(8,128)(2,1)} %bitcast.138, s32[1024]{0:T(1024)S(1)} %pad_clamp_fusion.3), kind=kCustom, calls=%fused_computation.4.clone | custom fusion | bytes 786440 | tf_op jit(solution)/shard_map/jit(_take)/gather | solution.py:69
  75.5 2.6 %gather_fusion.6 = bf16[2,128,768]{1,2,0:T(8,128)(2,1)S(1)} fusion(bf16[18,128,768]{1,2,0:T(8,128)(2,1)} %bitcast.139, s32[1024]{0:T(1024)S(1)} %pad_clamp_fusion.2), kind=kCustom, calls=%fused_computation.5.clone | custom fusion | bytes 786440 | tf_op jit(solution)/shard_map/jit(_take)/gather | solution.py:69
  78.1 2.6 %gather_fusion.7 = bf16[2,128,768]{1,2,0:T(8,128)(2,1)S(1)} fusion(bf16[18,128,768]{1,2,0:T(8,128)(2,1)} %bitcast.140, s32[1024]{0:T(1024)S(1)} %pad_clamp_fusion.1), kind=kCustom, calls=%fused_computation.6.clone | custom fusion | bytes 786440 | tf_op jit(solution)/shard_map/jit(_take)/gather | solution.py:69
  80.7 2.6 %gather_fusion = bf16[4,128,768]{2,1,0:T(8,128)(2,1)S(1)} fusion(bf16[18,128,768]{2,1,0:T(8,128)(2,1)} %copy.71, s32[1024]{0:T(1024)S(1)} %pad_clamp_fusion), kind=kCustom, calls=%fused_computation.7 | custom fusion | bytes 1572880 | tf_op jit(solution)/shard_map/jit(_take)/gather | solution.py:79
  83.3 0.5 convolution_bitcast_fusion
  83.9 0.6 copy.73
  84.5 0.6 fusion.99
  85.1 0.6 fusion.97
  85.6 0.6 fusion.95
  87.2 0.8 copy-done.3
  88.7 0.8 copy-done.2
  90.3 0.8 copy-done.1
  94.9 0.7 fusion.126
  95.7 1.9 %collective-permute-start.8 = (bf16[256,1280]{1,0:T(8,128)(2,1)S(1)}, bf16[256,1280]{1,0:T(8,128)(2,1)S(1)}, u32[]{:S(2)}, u32[]{:S(2)}) collective-permute-start(bf16[256,1280]{1,0:T(8,128)(2,1)S(1)} %get-tuple-element.354), channel_id=1, source_target_pairs={{0,4},{4,8},{8,12},{12,16},{16,20},{20,24},{24,28},{28,32},{32,36}... | collective-permute-start | bytes 1966088 | tf_op jit(solution)/shard_map/ppermute | solution.py:25
  97.6 0.6 compare_reduce_fusion.1
  98.3 0.7 compare_reduce_fusion
  98.9 5.7 %collective-permute-start.9 = (bf16[256,1280]{1,0:T(8,128)(2,1)S(1)}, bf16[256,1280]{1,0:T(8,128)(2,1)S(1)}, u32[]{:S(2)}, u32[]{:S(2)}) collective-permute-start(bf16[256,1280]{1,0:T(8,128)(2,1)S(1)} %get-tuple-element.353), channel_id=1, source_target_pairs={{4,0},{8,4},{12,8},{16,12},{20,16},{24,20},{28,24},{32,28},{36,32}... | collective-permute-start | bytes 1966088 | tf_op jit(solution)/shard_map/ppermute | solution.py:25
  104.7 5.0 %collective-permute-done.8 = bf16[256,1280]{1,0:T(8,128)(2,1)S(1)} collective-permute-done((bf16[256,1280]{1,0:T(8,128)(2,1)S(1)}, bf16[256,1280]{1,0:T(8,128)(2,1)S(1)}, u32[]{:S(2)}, u32[]{:S(2)}) %collective-permute-start.8) | collective-permute-done | bytes 655392 | tf_op jit(solution)/shard_map/ppermute | solution.py:25
  109.7 0.7 convert_select_fusion
  110.6 1.1 fusion.9
  111.7 1.1 collective-permute-done.9
  113.1 14.0 %all_to_all.5 = bf16[4,64,1792]{2,1,0:T(8,128)(2,1)S(1)} all-to-all(bf16[4,64,1792]{2,1,0:T(8,128)(2,1)S(1)} %bitcast.141), channel_id=1, replica_groups=mesh['slab'=128,'cross'=4] {'cross'}, dimensions={0} | all-to-all | bytes 1835008 | tf_op jit(solution)/shard_map/all_to_all | solution.py:36
  127.1 0.9 convert_reduce_fusion
  (79 shorter events, 7.5 us)
Async XLA Ops:
  0.0 83.3 %copy-start = (bf16[4,128,128]{2,1,0:T(8,128)(2,1)S(1)}, bf16[4,128,128]{2,1,0:T(8,128)(2,1)}, u32[]{:S(2)}) copy-start(bf16[4,128,128]{2,1,0:T(8,128)(2,1)} %param.65) | copy-start | bytes 393220
  1.1 24.4 %collective-permute-start = (bf16[1,1,2,3,128,128]{5,3,4,2,1,0:T(4,128)(2,1)S(1)}, bf16[1,1,2,3,128,128]{5,3,4,2,1,0:T(4,128)(2,1)S(1)}, u32[]{:S(2)}, u32[]{:S(2)}) collective-permute-start(bf16[1,1,2,3,128,128]{5,3,4,2,1,0:T(4,128)(2,1)S(1)} %bitcast.144), channel_id=1, source_target_pairs={{0,4},{4,8},{8,12},{12,16},{16,20},{20,24},{24,28},{28,32},{32,36}... | collective-permute-start | bytes 589832 | tf_op jit(solution)/shard_map/ppermute | solution.py:14
  3.1 22.5 %collective-permute-start.1 = (bf16[1,1,2,3,128,128]{5,3,4,2,1,0:T(4,128)(2,1)S(1)}, bf16[1,1,2,3,128,128]{5,3,4,2,1,0:T(4,128)(2,1)S(1)}, u32[]{:S(2)}, u32[]{:S(2)}) collective-permute-start(bf16[1,1,2,3,128,128]{5,3,4,2,1,0:T(4,128)(2,1)S(1)} %bitcast.145), channel_id=1, source_target_pairs={{4,0},{8,4},{12,8},{16,12},{20,16},{24,20},{28,24},{32,28},{36,32}... | collective-permute-start | bytes 589832 | tf_op jit(solution)/shard_map/ppermute | solution.py:17
  15.0 16.6 %collective-permute-start.4 = (bf16[1,1,2,3,6]{4,3,2,1,0:T(4,128)(2,1)S(1)}, bf16[1,1,2,3,6]{4,3,2,1,0:T(4,128)(2,1)S(1)}, u32[]{:S(2)}, u32[]{:S(2)}) collective-permute-start(bf16[1,1,2,3,6]{4,3,2,1,0:T(4,128)(2,1)S(1)} %fusion.93), channel_id=1, source_target_pairs={{0,4},{4,8},{8,12},{12,16},{16,20},{20,24},{24,28},{28,32},{32,36}... | collective-permute-start | bytes 224 | tf_op jit(solution)/shard_map/ppermute | solution.py:14
  16.9 14.7 %collective-permute-start.5 = (bf16[1,1,2,3,6]{4,3,2,1,0:T(4,128)(2,1)S(1)}, bf16[1,1,2,3,6]{4,3,2,1,0:T(4,128)(2,1)S(1)}, u32[]{:S(2)}, u32[]{:S(2)}) collective-permute-start(bf16[1,1,2,3,6]{4,3,2,1,0:T(4,128)(2,1)S(1)} %fusion.93), channel_id=1, source_target_pairs={{4,0},{8,4},{12,8},{16,12},{20,16},{24,20},{28,24},{32,28},{36,32}... | collective-permute-start | bytes 224 | tf_op jit(solution)/shard_map/ppermute | solution.py:17
  25.5 5.6 %copy-start.5 = (bf16[2,3,128,128]{3,2,1,0:T(8,128)(2,1)S(1)}, bf16[2,3,128,128]{3,2,1,0:T(8,128)(2,1)}, u32[]{:S(2)}) copy-start(bf16[2,3,128,128]{3,2,1,0:T(8,128)(2,1)} %param.68) | copy-start | bytes 589828
  25.5 5.6 %copy-start.8 = (s32[2,3]{1,0:T(2,128)S(1)}, s32[2,3]{1,0:T(2,128)}, u32[]{:S(2)}) copy-start(s32[2,3]{1,0:T(2,128)} %param.69) | copy-start | bytes 76
  26.4 12.9 %collective-permute-start.2 = (bf16[3,1,2,3,128,128]{5,4,3,2,1,0:T(8,128)(2,1)S(1)}, bf16[3,1,2,3,128,128]{5,4,3,2,1,0:T(8,128)(2,1)S(1)}, u32[]{:S(2)}, u32[]{:S(2)}) collective-permute-start(bf16[3,1,2,3,128,128]{5,4,3,2,1,0:T(8,128)(2,1)S(1)} %copy.52), channel_id=1, source_target_pairs={{0,1},{1,2},{2,3},{4,5},{5,6},{6,7},{8,9},{9,10},{10,11},{12,13},{... | collective-permute-start | bytes 1769480 | tf_op jit(solution)/shard_map/ppermute | solution.py:14
  29.8 13.6 %collective-permute-start.3 = (bf16[3,1,2,3,128,128]{5,4,3,2,1,0:T(8,128)(2,1)S(1)}, bf16[3,1,2,3,128,128]{5,4,3,2,1,0:T(8,128)(2,1)S(1)}, u32[]{:S(2)}, u32[]{:S(2)}) collective-permute-start(bf16[3,1,2,3,128,128]{5,4,3,2,1,0:T(8,128)(2,1)S(1)} %copy.52), channel_id=1, source_target_pairs={{1,0},{2,1},{3,2},{5,4},{6,5},{7,6},{9,8},{10,9},{11,10},{13,12},{... | collective-permute-start | bytes 1769480 | tf_op jit(solution)/shard_map/ppermute | solution.py:17
  31.7 12.2 %collective-permute-start.6 = (bf16[3,1,2,3,6]{4,3,2,1,0:T(4,128)(2,1)S(1)}, bf16[3,1,2,3,6]{4,3,2,1,0:T(4,128)(2,1)S(1)}, u32[]{:S(2)}, u32[]{:S(2)}) collective-permute-start(bf16[3,1,2,3,6]{4,3,2,1,0:T(4,128)(2,1)S(1)} %pad_maximum_fusion.1), channel_id=1, source_target_pairs={{0,1},{1,2},{2,3},{4,5},{5,6},{6,7},{8,9},{9,10},{10,11},{12,13},{... | collective-permute-start | bytes 656 | tf_op jit(solution)/shard_map/ppermute | solution.py:14
  36.2 7.7 %collective-permute-start.7 = (bf16[3,1,2,3,6]{4,3,2,1,0:T(4,128)(2,1)S(1)}, bf16[3,1,2,3,6]{4,3,2,1,0:T(4,128)(2,1)S(1)}, u32[]{:S(2)}, u32[]{:S(2)}) collective-permute-start(bf16[3,1,2,3,6]{4,3,2,1,0:T(4,128)(2,1)S(1)} %pad_maximum_fusion.1), channel_id=1, source_target_pairs={{1,0},{2,1},{3,2},{5,4},{6,5},{7,6},{9,8},{10,9},{11,10},{13,12},{... | collective-permute-start | bytes 656 | tf_op jit(solution)/shard_map/ppermute | solution.py:17
  83.3 1.1 copy-start.7
  85.0 1.1 copy-start.4
  85.1 1.1 copy-start.6
  87.0 1.0 copy-start.3
  88.5 1.0 copy-start.2
  90.1 1.0 copy-start.1
  95.7 14.0 %collective-permute-start.8 = (bf16[256,1280]{1,0:T(8,128)(2,1)S(1)}, bf16[256,1280]{1,0:T(8,128)(2,1)S(1)}, u32[]{:S(2)}, u32[]{:S(2)}) collective-permute-start(bf16[256,1280]{1,0:T(8,128)(2,1)S(1)} %get-tuple-element.354), channel_id=1, source_target_pairs={{0,4},{4,8},{8,12},{12,16},{16,20},{20,24},{24,28},{28,32},{32,36}... | collective-permute-start | bytes 1966088 | tf_op jit(solution)/shard_map/ppermute | solution.py:25
  98.9 13.8 %collective-permute-start.9 = (bf16[256,1280]{1,0:T(8,128)(2,1)S(1)}, bf16[256,1280]{1,0:T(8,128)(2,1)S(1)}, u32[]{:S(2)}, u32[]{:S(2)}) collective-permute-start(bf16[256,1280]{1,0:T(8,128)(2,1)S(1)} %get-tuple-element.353), channel_id=1, source_target_pairs={{4,0},{8,4},{12,8},{16,12},{20,16},{24,20},{28,24},{32,28},{36,32}... | collective-permute-start | bytes 1966088 | tf_op jit(solution)/shard_map/ppermute | solution.py:25
where the time goes:
time: 129 us; the launch traced here: 128 us
  local copies, waits for them, and re-layouts  43 us (33%)
  starting transfers between devices  39.2 us (30%)
  blocking collectives  14 us (11%)
  waiting for transfers between devices  11.3 us (9%)
  other arithmetic  10.8 us (8%)
  matrix products  9.05 us (7%)
    gather x7, local copies, waits for them, and re-layouts, body(): rows = jnp.take(extended, a_cols[:, k_index], axis=0)  21.3 us
    ppermute x4, starting transfers between devices, with_halo(): lax.ppermute(lax.slice_in_dim(block, 0, width, axis=dim), axis, backward)  19.7 us
    all_to_all x1, blocking collectives, sent_and_summed(): lax.all_to_all(split_up(value, dim, devices), axis, 0, 0, tiled=True)  14 us
    ppermute x4, starting transfers between devices, with_halo(): lax.ppermute(lax.slice_in_dim(block, block.shape[dim] - width, None, axis...  11.8 us
    ppermute x2, starting transfers between devices, from_behind(): return lax.ppermute(value, axis, pairs)  7.66 us
    convert_element_type x1, local copies, waits for them, and re-layouts, body(): extended.astype(jnp.bfloat16).reshape(9 * blocks, tile_size, wide)  6.6 us
    ppermute x2, waiting for transfers between devices, from_behind(): return lax.ppermute(value, axis, pairs)  6.09 us
    reshape x1, local copies, waits for them, and re-layouts, body(): extended.astype(jnp.bfloat16).reshape(9 * blocks, tile_size, wide)  5.76 us
  transfers between devices with their start and end apart: 10, of which 4 were waited for; matrix products, arithmetic and copies ran while one was open for 7% of the time, Pallas kernels for 0%

commit v1 on v0

v1 whole, which is shorter than its diff:
```python
import functools

import jax
import jax.numpy as jnp
from jax import lax
from jax.experimental import pallas as pl
from jax.experimental.pallas import tpu as pltpu
from jax.sharding import PartitionSpec as P

CB = 2
TILE = 128
NB = 2
KP = 3
K = 7
OV = 4
WIDTH = CB * TILE
WIDE = 3 * WIDTH
PW = 5 * WIDTH
CW = 7 * WIDTH
HALF = CW // 2
TROWS = NB * KP * TILE
CROWS = NB * KP * 16
BROWS = TROWS + CROWS
F32 = jnp.float32
BF16 = jnp.bfloat16

OWN_R, OWN_L, OWN_NEAR, OWN_FAR, REL_L_NEAR, REL_L_FAR, REL_R_NEAR, REL_R_FAR = range(8)
FAR0, NEAR0 = 8, 12
X2A, X2B, X1D, X1S, X3D, X3S = range(16, 22)
N_SEMS = 22


def dot(a, b):
    return lax.dot_general(a, b, (((1,), (0,)), ((), ())), preferred_element_type=F32)


def kernel(
    n_slab, n_cross,
    a_hbm, o_hbm, p_hbm, a_cols, over_rows, over_cols, p_cols,
    out_ref,
    halo, dense, a_in, o_in, a_dense, p_turned, o_lhs, o_rhs, acc, prod,
    send_far, send_near, recv_far, recv_near, total,
    x_send, x_recv, local_sem, send_sem, recv_sem,
):
    s = lax.axis_index("slab")
    c = lax.axis_index("cross")
    core = lax.rem(s, 2)
    near = s + 1 - 2 * core
    far = s - 1 + 2 * core
    far_ok = jnp.logical_and(far >= 0, far < n_slab)
    right = lax.rem(c + 1, n_cross)
    left = lax.rem(c + n_cross - 1, n_cross)
    has_l = c > 0
    has_r = c < n_cross - 1
    r_near = 2 - 2 * core
    r_far = 2 * core
    rows = CW // 7 // n_cross

    def device(slab, cross):
        return {"slab": slab, "cross": cross}

    def remote(src, dst, i, slab, cross):
        return pltpu.make_async_remote_copy(
            src_ref=src, dst_ref=dst, send_sem=send_sem.at[i], recv_sem=recv_sem.at[i],
            device_id=device(slab, cross), device_id_type=pl.DeviceIdType.MESH,
        )

    load_p = pltpu.make_async_copy(p_hbm, halo.at[4, pl.ds(0, TROWS)], local_sem.at[0])
    load_a = pltpu.make_async_copy(a_hbm, a_in.at[:, pl.ds(0, K)], local_sem.at[1])
    load_o = pltpu.make_async_copy(o_hbm, o_in, local_sem.at[2])
    load_p.start()
    load_a.start()
    load_o.start()

    barrier = pltpu.get_barrier_semaphore()

    def greet(slab, cross):
        pl.semaphore_signal(
            barrier, inc=1, device_id=device(slab, cross), device_id_type=pl.DeviceIdType.MESH
        )

    greet(near, c)
    greet(s, left)
    greet(s, right)

    @pl.when(far_ok)
    def _():
        greet(far, c)

    for n in range(NB):
        for m in range(KP):
            number = p_cols[n, m].astype(F32)
            halo[4, pl.ds(TROWS + (n * KP + m) * 16, 16), :] = jnp.full((16, TILE), number).astype(BF16)

    nothing = jnp.full((CROWS, TILE), -1.0, BF16)

    def leave_out(b):
        halo[b, pl.ds(TROWS, CROWS), :] = nothing

    @pl.when(jnp.logical_not(has_l))
    def _():
        for r in range(3):
            leave_out(3 * r)

    @pl.when(jnp.logical_not(has_r))
    def _():
        for r in range(3):
            leave_out(3 * r + 2)

    @pl.when(jnp.logical_not(far_ok))
    def _():
        for u in range(3):
            leave_out(3 * r_far + u)
        recv_far[...] = jnp.zeros_like(recv_far)

    for n in range(NB):
        a_in[n, K] = jnp.zeros((TILE, TILE), BF16)
    acc[...] = jnp.zeros_like(acc)
    total[...] = jnp.zeros_like(total)

    pl.semaphore_wait(barrier, 3 + far_ok.astype(jnp.int32))
    load_p.wait()

    own_r = remote(halo.at[4], halo.at[3], OWN_R, s, right)
    own_l = remote(halo.at[4], halo.at[5], OWN_L, s, left)
    own_near = remote(halo.at[4], halo.at[3 * r_far + 1], OWN_NEAR, near, c)
    own_far = remote(halo.at[4], halo.at[3 * r_near + 1], OWN_FAR, far, c)
    rel_l_near = remote(halo.at[3], halo.at[3 * r_far], REL_L_NEAR, near, c)
    rel_l_far = remote(halo.at[3], halo.at[3 * r_near], REL_L_FAR, far, c)
    rel_r_near = remote(halo.at[5], halo.at[3 * r_far + 2], REL_R_NEAR, near, c)
    rel_r_far = remote(halo.at[5], halo.at[3 * r_near + 2], REL_R_FAR, far, c)

    @pl.when(has_r)
    def _():
        own_r.start()

    @pl.when(has_l)
    def _():
        own_l.start()

    @pl.when(far_ok)
    def _():
        own_far.start()

    own_near.start()

    def densify(b):
        for n in range(NB):
            tiles, marks = [], []
            for m in range(KP):
                i = n * KP + m
                tiles.append(halo[b, pl.ds(i * TILE, TILE), :].reshape(8, 16, TILE))
                marks.append(halo[b, pl.ds(TROWS + i * 16, 16), :])
            for q in range(3 * CB):
                value = jnp.zeros((8, 16, TILE), BF16)
                for m in range(KP):
                    here = jnp.broadcast_to((marks[m] == jnp.asarray(q, BF16))[None], value.shape)
                    value = jnp.where(here, tiles[m], value)
                dense[2 * b + n, :, pl.ds(q * TILE, TILE)] = value.reshape(TILE, TILE)

    densify(4)
    for n in range(NB):
        for q in range(3 * CB):
            block = dense[8 + n, :, pl.ds(q * TILE, TILE)]
            p_turned[pl.ds(q * TILE, TILE), pl.ds(n * TILE, TILE)] = block.T

    load_a.wait()
    load_o.wait()
    for n in range(NB):
        for t in range(18):
            at = jnp.int32(K)
            for k in range(K):
                at = jnp.where(a_cols[n, k] == t, k, at)
            a_dense[t // 6, pl.ds(n * TILE, TILE), pl.ds((t % 6) * TILE, TILE)] = a_in[n, at]
        for o in range(OV):
            o_lhs[pl.ds(n * TILE, TILE), pl.ds(o * TILE, TILE)] = jnp.where(
                over_rows[o] == n, o_in[o], jnp.zeros((TILE, TILE), BF16)
            )

    @pl.when(has_l)
    def _():
        own_r.wait_recv()
        rel_l_near.start()

        @pl.when(far_ok)
        def _():
            rel_l_far.start()

    @pl.when(has_r)
    def _():
        own_l.wait_recv()
        rel_r_near.start()

        @pl.when(far_ok)
        def _():
            rel_r_far.start()

    def add_slab(r):
        for j in range(3):
            right_side = dense[pl.ds(6 * r, 6), :, pl.ds(j * WIDTH, WIDTH)].reshape(WIDE, WIDTH)
            at = pl.ds(pl.multiple_of((r + j) * WIDTH, WIDTH), WIDTH)
            acc[:, at] += dot(a_dense[r], right_side)

    densify(3)
    densify(5)
    add_slab(1)

    own_near.wait_recv()

    @pl.when(has_l)
    def _():
        rel_l_near.wait_recv()

    @pl.when(has_r)
    def _():
        rel_r_near.wait_recv()

    for u in range(3):
        densify(3 * r_near + u)
    add_slab(r_near)

    @pl.when(far_ok)
    def _():
        own_far.wait_recv()

        @pl.when(has_l)
        def _():
            rel_l_far.wait_recv()

        @pl.when(has_r)
        def _():
            rel_r_far.wait_recv()

    for u in range(3):
        densify(3 * r_far + u)
    add_slab(r_far)

    for o in range(OV):
        t = over_cols[o]
        shift = (t >= 6).astype(jnp.int32) + (t >= 12).astype(jnp.int32)
        for j in range(5 * CB):
            value = jnp.zeros((TILE, TILE), BF16)
            for r in range(3):
                if 0 <= j - CB * r < 3 * CB:
                    value = jnp.where(shift == r, dense[t, :, pl.ds((j - CB * r) * TILE, TILE)], value)
            o_rhs[pl.ds(o * TILE, TILE), pl.ds(j * TILE, TILE)] = value

    for j in range(5):
        at = pl.ds(j * WIDTH, WIDTH)
        prod[:, at] = (acc[:, at] + dot(o_lhs[...], o_rhs[:, at])).astype(BF16)

    def block_rows(q):
        return p_turned[pl.ds(pl.multiple_of(q * WIDTH, WIDTH), WIDTH), :]

    order = [lax.rem(c + off, n_cross) for off in (2, 1, 3, 0)]

    def partial(q, send):
        lhs = block_rows(q)
        for j in range(5):
            at = pl.ds(j * WIDTH, WIDTH)
            send[:, :, at] = dot(lhs, prod[:, at]).astype(BF16).reshape(n_cross, rows, WIDTH)

    partial(r_far, send_far)
    far_copies = [remote(send_far.at[i], recv_far.at[i], FAR0 + k, far, c) for k, i in enumerate(order)]

    @pl.when(far_ok)
    def _():
        for copy in far_copies:
            copy.start()

    partial(r_near, send_near)
    near_copies = [remote(send_near.at[i], recv_near.at[i], NEAR0 + k, near, c) for k, i in enumerate(order)]
    for copy in near_copies:
        copy.start()

    lhs = block_rows(1)
    for j in range(5):
        total[:, :, pl.ds((j + 1) * WIDTH, WIDTH)] = dot(lhs, prod[:, pl.ds(j * WIDTH, WIDTH)]).reshape(
            n_cross, rows, WIDTH
        )

    near_at = pl.ds(pl.multiple_of((2 - 2 * core) * WIDTH, WIDTH), PW)
    far_at = pl.ds(pl.multiple_of(2 * core * WIDTH, WIDTH), PW)

    def owned(k):
        i = order[k]
        near_copies[k].wait_recv()
        total[i, :, near_at] += recv_near[i].astype(F32)

        @pl.when(far_ok)
        def _():
            far_copies[k].wait_recv()

        total[i, :, far_at] += recv_far[i].astype(F32)
        return i

    low, high = pl.ds(0, HALF), pl.ds(HALF, HALF)

    def x_copy(i, cross):
        return remote(x_send.at[i - X2A], x_recv.at[i - X2A], i, s, cross)

    x2a, x2b = x_copy(X2A, right), x_copy(X2B, left)
    x1d, x1s = x_copy(X1D, right), x_copy(X1S, right)
    x3d, x3s = x_copy(X3D, left), x_copy(X3S, left)

    i = owned(0)
    x_send[0] = total[i, :, low].astype(BF16)
    x_send[1] = total[i, :, high].astype(BF16)
    x2a.start()
    x2b.start()
    i_next = owned(1)
    x_send[2] = total[i_next, :, high].astype(BF16)
    x1d.start()
    i_last = owned(2)
    x_send[4] = total[i_last, :, low].astype(BF16)
    x3d.start()
    x2a.wait_recv()
    x_send[3] = (total[i_next, :, low] + x_recv[0].astype(F32)).astype(BF16)
    x1s.start()
    x2b.wait_recv()
    x_send[5] = (total[i_last, :, high] + x_recv[1].astype(F32)).astype(BF16)
    x3s.start()
    i = owned(3)
    x1d.wait_recv()
    x3d.wait_recv()
    x1s.wait_recv()
    out_ref[:, low] = total[i, :, low] + x_recv[3].astype(F32) + x_recv[4].astype(F32)
    x3s.wait_recv()
    out_ref[:, high] = total[i, :, high] + x_recv[2].astype(F32) + x_recv[5].astype(F32)

    own_near.wait_send()
    for copy in near_copies + [x2a, x2b, x1d, x1s, x3d, x3s]:
        copy.wait_send()

    @pl.when(has_r)
    def _():
        own_r.wait_send()
        rel_r_near.wait_send()

    @pl.when(has_l)
    def _():
        own_l.wait_send()
        rel_l_near.wait_send()

    @pl.when(far_ok)
    def _():
        own_far.wait_send()
        for copy in far_copies:
            copy.wait_send()

        @pl.when(has_r)
        def _():
            rel_r_far.wait_send()

        @pl.when(has_l)
        def _():
            rel_l_far.wait_send()


def body(n_slab, n_cross, a_tiles, a_cols, over_tiles, over_rows, over_cols, p_tiles, p_cols):
    rows = CB * TILE // n_cross
    hbm = pl.BlockSpec(memory_space=pl.ANY)
    smem = pl.BlockSpec(memory_space=pltpu.SMEM)
    return pl.pallas_call(
        functools.partial(kernel, n_slab, n_cross),
        out_shape=jax.ShapeDtypeStruct((rows, CW), F32),
        in_specs=[hbm, hbm, hbm, smem, smem, smem, smem],
        out_specs=pl.BlockSpec(memory_space=pltpu.VMEM),
        scratch_shapes=[
            pltpu.VMEM((9, BROWS, TILE), BF16),
            pltpu.VMEM((18, TILE, WIDE), BF16),
            pltpu.VMEM((NB, K + 1, TILE, TILE), BF16),
            pltpu.VMEM((OV, TILE, TILE), BF16),
            pltpu.VMEM((3, NB * TILE, WIDE), BF16),
            pltpu.VMEM((WIDE, NB * TILE), BF16),
            pltpu.VMEM((NB * TILE, OV * TILE), BF16),
            pltpu.VMEM((OV * TILE, PW), BF16),
            pltpu.VMEM((NB * TILE, PW), F32),
            pltpu.VMEM((NB * TILE, PW), BF16),
            pltpu.VMEM((n_cross, rows, PW), BF16),
            pltpu.VMEM((n_cross, rows, PW), BF16),
            pltpu.VMEM((n_cross, rows, PW), BF16),
            pltpu.VMEM((n_cross, rows, PW), BF16),
            pltpu.VMEM((n_cross, rows, CW), F32),
            pltpu.VMEM((6, rows, HALF), BF16),
            pltpu.VMEM((6, rows, HALF), BF16),
            pltpu.SemaphoreType.DMA((3,)),
            pltpu.SemaphoreType.DMA((N_SEMS,)),
            pltpu.SemaphoreType.DMA((N_SEMS,)),
        ],
        compiler_params=pltpu.CompilerParams(collective_id=0, has_side_effects=True),
    )(a_tiles, over_tiles, p_tiles.reshape(TROWS, TILE), a_cols, over_rows, over_cols, p_cols)


def solution(mesh):
    return jax.shard_map(
        functools.partial(body, mesh.shape["slab"], mesh.shape["cross"]),
        mesh=mesh,
        in_specs=(
            P(("slab", "cross"), None, None, None),
            P(("slab", "cross"), None),
            P(("slab", "cross"), None, None),
            P(("slab", "cross")),
            P(("slab", "cross")),
            P(("slab", "cross"), None, None, None),
            P(("slab", "cross"), None),
        ),
        out_specs=P(("slab", "cross"), None),
        check_vma=False,
    )
```

time: 129 us -> 43.5 us (0.34)
  Pallas kernels: 0 us -> 41.5 us
  local copies, waits for them, and re-layouts: 43 us -> 1.82 us
  starting transfers between devices: 39.2 us -> 0 us
  blocking collectives: 14 us -> 0 us
  waiting for transfers between devices: 11.3 us -> 0 us
  other arithmetic: 10.8 us -> 0 us
  matrix products: 9.05 us -> 0 us
    pallas_call x0 -> x1, Pallas kernels: none -> 41.5 us  [body(): pl.pallas_call(functools.partial(kernel, n_slab, n_cross), out_shape=jax....]
    ppermute x10 -> x0, starting transfers between devices: 39.2 us -> none  [the longest x4 19.7 us: with_halo(): lax.ppermute(lax.slice_in_dim(block, 0, width, axis=dim), axis, backward)]
    gather x8 -> x0, local copies, waits for them, and re-layouts: 23.9 us -> none  [the longest x7 21.3 us: body(): rows = jnp.take(extended, a_cols[:, k_index], axis=0)]
    all_to_all x1 -> x0, blocking collectives: 14 us -> none  [sent_and_summed(): lax.all_to_all(split_up(value, dim, devices), axis, 0, 0, tiled=True)]
    ppermute x10 -> x0, waiting for transfers between devices: 11.3 us -> none  [the longest x2 6.09 us: from_behind(): return lax.ppermute(value, axis, pairs)]
    dot_general x14 -> x0, matrix products: 9.05 us -> none  [the longest x1 3.14 us: body(): jnp.einsum('xynmq,xynmab->xynaqb', got_picks, got_tiles, preferred_elemen...]
    convert_element_type x1 -> x0, local copies, waits for them, and re-layouts: 6.6 us -> none  [body(): extended.astype(jnp.bfloat16).reshape(9 * blocks, tile_size, wide)]
    reshape x1 -> x0, local copies, waits for them, and re-layouts: 5.76 us -> none  [body(): extended.astype(jnp.bfloat16).reshape(9 * blocks, tile_size, wide)]
  transfers between devices with their start and end apart: 10 -> 0, of which waited for: 4 -> 0; matrix products, arithmetic and copies ran while one was open for 7% -> 0% of each run, Pallas kernels for 0% -> 0%
where the time goes in v1:
time: 43.5 us; the launch traced here: 43.3 us
  Pallas kernels  41.5 us (95%)
  local copies, waits for them, and re-layouts  1.82 us (4%)
    pallas_call x1, Pallas kernels, body(): pl.pallas_call(functools.partial(kernel, n_slab, n_cross), out_shape=jax....  41.5 us
    unnamed x1, local copies, waits for them, and re-layouts  1.82 us

profile of v1, /device:TPU:56, one launch (start us, length us, event | category | flops | bytes accessed | tf_op | source)
XLA Modules:
  0.0 43.3 jit_solution(15416558424011796586)
XLA Ops:
  0.0 41.5 %shard_map.73 = f32[64,1792]{1,0:T(8,128)} custom-call(bf16[2,7,128,128]{3,2,1,0:T(8,128)(2,1)} %a_hbm.1, bf16[4,128,128]{2,1,0:T(8,128)(2,1)} %o_hbm.1, bf16[768,128]{1,0:T(8,128)(2,1)} %bitcast.1, s32[2,7]{1,0:T(2,128)} %a_cols.1, s32[4]{0:T(128)} %over_rows.1, s32[4]{0:T(128)} %over_cols.1, s32[2,3]{1,0:T(2,128)} %p_cols.1), custom_call_target="tpu_custom_call" | custom-call | tf_op jit(solution)/shard_map/pallas_call | solution.py:364
  41.5 1.8 %copy.9 = f32[64,1792]{1,0:T(8,128)} copy(f32[64,1792]{1,0:T(8,128)} %shard_map.73) | data formatting | bytes 917504

commit v2 on v1

v2 whole, which is shorter than its diff:
```python
import functools

import jax
import jax.numpy as jnp
from jax import lax
from jax.experimental import pallas as pl
from jax.experimental.pallas import tpu as pltpu
from jax.sharding import PartitionSpec as P

CB = 2
TILE = 128
NB = 2
KP = 3
K = 7
OV = 4
WIDTH = CB * TILE
WIDE = 3 * WIDTH
PW = 5 * WIDTH
CW = 7 * WIDTH
EARLY = CW - PW
NCH = 3
TPC = NB * KP // NCH
TROWS = TPC * TILE
BROWS = TROWS + 16
F32 = jnp.float32
BF16 = jnp.bfloat16

OWN_R, OWN_L, OWN_NEAR, OWN_FAR, REL_L_NEAR, REL_L_FAR, REL_R_NEAR, REL_R_FAR = (NCH * i for i in range(8))
FAR0 = 8 * NCH
NEAR0 = FAR0 + 5
X0 = NEAR0 + 4
N_SEMS = X0 + 16


def dot(a, b):
    return lax.dot_general(a, b, (((1,), (0,)), ((), ())), preferred_element_type=F32)


def kernel(
    n_slab, n_cross,
    a_hbm, o_hbm, p_hbm, a_cols, over_rows, over_cols, p_cols,
    out_ref,
    halo, dense, a_in, o_in, a_dense, p_turned, acc, prod,
    send_far, send_near, recv_far, recv_near, total,
    e_send, e_recv, x_send, x_recv, local_sem, send_sem, recv_sem,
):
    s = lax.axis_index("slab")
    c = lax.axis_index("cross")
    core = lax.rem(s, 2)
    near = s + 1 - 2 * core
    far = s - 1 + 2 * core
    far_ok = jnp.logical_and(far >= 0, far < n_slab)
    right = lax.rem(c + 1, n_cross)
    left = lax.rem(c + n_cross - 1, n_cross)
    has_l = c > 0
    has_r = c < n_cross - 1
    r_near = 2 - 2 * core
    r_far = 2 * core
    rows = CB * TILE // n_cross
    part_rows = rows // 2

    def device(slab, cross):
        return {"slab": slab, "cross": cross}

    def remote(src, dst, i, slab, cross):
        return pltpu.make_async_remote_copy(
            src_ref=src, dst_ref=dst, send_sem=send_sem.at[i], recv_sem=recv_sem.at[i],
            device_id=device(slab, cross), device_id_type=pl.DeviceIdType.MESH,
        )

    load_p = [
        pltpu.make_async_copy(
            p_hbm.at[pl.ds(h * TROWS, TROWS)], halo.at[4, h, pl.ds(0, TROWS)], local_sem.at[2 + h]
        )
        for h in range(NCH)
    ]
    load_a = pltpu.make_async_copy(a_hbm, a_in.at[:, pl.ds(0, K)], local_sem.at[0])
    load_o = pltpu.make_async_copy(o_hbm, o_in.at[pl.ds(0, OV)], local_sem.at[1])
    for load in load_p + [load_a, load_o]:
        load.start()

    barrier = pltpu.get_barrier_semaphore()

    def greet(slab, cross):
        pl.semaphore_signal(
            barrier, inc=1, device_id=device(slab, cross), device_id_type=pl.DeviceIdType.MESH
        )

    @pl.when(far_ok)
    def _():
        greet(far, c)

    greet(s, left)
    greet(s, right)
    greet(near, c)

    row = lax.broadcasted_iota(jnp.int32, (16, TILE), 0)
    for h in range(NCH):
        value = jnp.full((16, TILE), -1.0, F32)
        for j in range(TPC):
            n, m = divmod(h * TPC + j, KP)
            value = jnp.where(row == j, p_cols[n, m].astype(F32), value)
        halo[4, h, pl.ds(TROWS, 16), :] = value.astype(BF16)

    nothing = jnp.full((16, TILE), -1.0, BF16)

    def leave_out(b):
        for h in range(NCH):
            halo[b, h, pl.ds(TROWS, 16), :] = nothing

    @pl.when(jnp.logical_not(has_l))
    def _():
        for r in range(3):
            leave_out(3 * r)

    @pl.when(jnp.logical_not(has_r))
    def _():
        for r in range(3):
            leave_out(3 * r + 2)

    @pl.when(jnp.logical_not(far_ok))
    def _():
        for u in range(3):
            leave_out(3 * r_far + u)
        recv_far[...] = jnp.zeros_like(recv_far)

    for n in range(NB):
        a_in[n, K] = jnp.zeros((TILE, TILE), BF16)
    o_in[OV] = jnp.zeros((TILE, TILE), BF16)
    acc[...] = jnp.zeros_like(acc)
    total[...] = jnp.zeros_like(total)

    pl.semaphore_wait(barrier, 3 + far_ok.astype(jnp.int32))

    def halo_copies(b, to, first, slab, cross):
        return [remote(halo.at[b, h], halo.at[to, h], first + h, slab, cross) for h in range(NCH)]

    own_r = halo_copies(4, 3, OWN_R, s, right)
    own_l = halo_copies(4, 5, OWN_L, s, left)
    own_near = halo_copies(4, 3 * r_far + 1, OWN_NEAR, near, c)
    own_far = halo_copies(4, 3 * r_near + 1, OWN_FAR, far, c)
    rel_l_near = halo_copies(3, 3 * r_far, REL_L_NEAR, near, c)
    rel_l_far = halo_copies(3, 3 * r_near, REL_L_FAR, far, c)
    rel_r_near = halo_copies(5, 3 * r_far + 2, REL_R_NEAR, near, c)
    rel_r_far = halo_copies(5, 3 * r_near + 2, REL_R_FAR, far, c)

    for h in range(NCH):
        load_p[h].wait()

        @pl.when(has_r)
        def _():
            own_r[h].start()

        @pl.when(has_l)
        def _():
            own_l[h].start()

        @pl.when(far_ok)
        def _():
            own_far[h].start()

        own_near[h].start()

    def densify(b):
        for n in range(NB):
            tiles, marks = [], []
            for m in range(KP):
                h, j = divmod(n * KP + m, TPC)
                tiles.append(halo[b, h, pl.ds(j * TILE, TILE), :].reshape(8, 16, TILE))
                number = halo[b, h, pl.ds(TROWS, 16), :].astype(F32)[j : j + 1]
                marks.append(jnp.broadcast_to(number, (16, TILE)).astype(BF16))
            for q in range(3 * CB):
                value = jnp.zeros((8, 16, TILE), BF16)
                for m in range(KP):
                    here = jnp.broadcast_to((marks[m] == jnp.asarray(q, BF16))[None], value.shape)
                    value = jnp.where(here, tiles[m], value)
                dense[2 * b + n, :, pl.ds(q * TILE, TILE)] = value.reshape(TILE, TILE)

    def place_a(r):
        for n in range(NB):
            for t in range(6 * r, 6 * r + 6):
                at = jnp.int32(K)
                for k in range(K):
                    at = jnp.where(a_cols[n, k] == t, k, at)
                value = a_in[n, at].astype(F32)
                for o in range(OV):
                    hit = jnp.logical_and(over_rows[o] == n, over_cols[o] == t)
                    value += o_in[jnp.where(hit, o, OV)].astype(F32)
                a_dense[r, pl.ds(n * TILE, TILE), pl.ds((t % 6) * TILE, TILE)] = value.astype(BF16)

    def relay(h):
        @pl.when(has_l)
        def _():
            own_r[h].wait_recv()

            @pl.when(far_ok)
            def _():
                rel_l_far[h].start()

            rel_l_near[h].start()

        @pl.when(has_r)
        def _():
            own_l[h].wait_recv()

            @pl.when(far_ok)
            def _():
                rel_r_far[h].start()

            rel_r_near[h].start()

    def product_of(r, u, count, j):
        right_side = dense[pl.ds(6 * r + 2 * u, 2 * count), :, pl.ds(j * WIDTH, WIDTH)]
        return dot(
            a_dense[r, :, pl.ds(u * WIDTH, count * WIDTH)], right_side.reshape(count * WIDTH, WIDTH)
        )

    def columns(r, j):
        return pl.ds(pl.multiple_of((r + j) * WIDTH, WIDTH), WIDTH)

    def add_blocks(r, u, count):
        for j in range(3):
            acc[:, columns(r, j)] += product_of(r, u, count, j)

    densify(4)
    for n in range(NB):
        for q in range(3 * CB):
            block = dense[8 + n, :, pl.ds(q * TILE, TILE)]
            p_turned[pl.ds(q * TILE, TILE), pl.ds(n * TILE, TILE)] = block.T
    load_a.wait()
    load_o.wait()
    place_a(1)
    relay(0)
    place_a(0)
    relay(1)
    place_a(2)
    for h in range(2, NCH):
        relay(h)
    densify(3)
    densify(5)
    add_blocks(1, 0, 3)

    for h in range(NCH):
        own_near[h].wait_recv()

    @pl.when(has_l)
    def _():
        for h in range(NCH):
            rel_l_near[h].wait_recv()

    @pl.when(has_r)
    def _():
        for h in range(NCH):
            rel_r_near[h].wait_recv()

    for u in range(3):
        densify(3 * r_near + u)
    add_blocks(r_near, 0, 3)
    for j in range(2):
        at = pl.ds(pl.multiple_of((3 - 3 * core + j) * WIDTH, WIDTH), WIDTH)
        prod[:, at] = acc[:, at].astype(BF16)

    @pl.when(far_ok)
    def _():
        for h in range(NCH):
            own_far[h].wait_recv()

    densify(3 * r_far + 1)
    add_blocks(r_far, 1, 1)

    @pl.when(jnp.logical_and(far_ok, has_l))
    def _():
        for h in range(NCH):
            rel_l_far[h].wait_recv()

    densify(3 * r_far)
    add_blocks(r_far, 0, 1)

    @pl.when(jnp.logical_and(far_ok, has_r))
    def _():
        for h in range(NCH):
            rel_r_far[h].wait_recv()

    densify(3 * r_far + 2)
    for j in range(3):
        at = columns(r_far, j)
        prod[:, at] = (acc[:, at] + product_of(r_far, 2, 1, j)).astype(BF16)

    order = [lax.rem(c + off, n_cross) for off in (2, 1, 3, 0)]

    def chunk_of(q, k, j):
        lhs = p_turned[pl.ds(pl.multiple_of(q * WIDTH + order[k] * rows, rows), rows), :]
        return dot(lhs, prod[:, pl.ds(j * WIDTH, WIDTH)])

    first_half, second_half = pl.ds(0, part_rows), pl.ds(part_rows, part_rows)
    far_copies = [
        remote(send_far.at[0, half], recv_far.at[0, half], FAR0 + i, far, c)
        for i, half in enumerate((first_half, second_half))
    ]
    far_copies += [remote(send_far.at[k], recv_far.at[k], FAR0 + 1 + k, far, c) for k in range(1, 4)]
    near_copies = [remote(send_near.at[k], recv_near.at[k], NEAR0 + k, near, c) for k in range(4)]

    def send_far_chunk(k):
        for j in range(5):
            send_far[k, :, pl.ds(j * WIDTH, WIDTH)] = chunk_of(r_far, k, j).astype(BF16)

        @pl.when(far_ok)
        def _():
            for copy in far_copies[:2] if k == 0 else [far_copies[k + 1]]:
                copy.start()

    def send_near_chunk(k):
        for j in range(5):
            send_near[k, :, pl.ds(j * WIDTH, WIDTH)] = chunk_of(r_near, k, j).astype(BF16)
        near_copies[k].start()

    def own_chunk(k):
        for j in range(5):
            total[k, :, pl.ds((j + 1) * WIDTH, WIDTH)] = chunk_of(1, k, j)

    send_far_chunk(0)
    send_near_chunk(0)
    send_far_chunk(1)
    send_near_chunk(1)
    send_near_chunk(2)
    own_chunk(0)
    send_far_chunk(2)
    send_far_chunk(3)
    send_near_chunk(3)
    for k in range(1, 4):
        own_chunk(k)

    near_at = pl.ds(pl.multiple_of((2 - 2 * core) * WIDTH, WIDTH), PW)
    far_at = pl.ds(pl.multiple_of(2 * core * WIDTH, WIDTH), PW)
    everything = pl.ds(0, rows)

    def add_near(k):
        near_copies[k].wait_recv()
        total[k, :, near_at] += recv_near[k].astype(F32)

    def add_far(k, i, here):
        @pl.when(far_ok)
        def _():
            far_copies[i].wait_recv()

        total[k, here, far_at] += recv_far[k, here, :].astype(F32)

    early_first = pl.multiple_of((5 - 5 * core) * WIDTH, WIDTH)
    late_first = pl.multiple_of(2 * core * WIDTH, WIDTH)
    early = [pl.ds(pl.multiple_of(early_first + i * (EARLY // 2), TILE), EARLY // 2) for i in range(2)]
    late = [pl.ds(pl.multiple_of(late_first + i * (PW // 2), TILE), PW // 2) for i in range(2)]

    to = [right, left]

    def early_copy(step, side):
        i = 2 * step + side
        return remote(e_send.at[i], e_recv.at[i], X0 + i, s, to[side])

    def late_copy(step, side, here, extra):
        i = 2 * step + side
        return remote(x_send.at[i, here], x_recv.at[i, here], X0 + 6 + extra + side, s, to[side])

    e = [[early_copy(step, side) for side in range(2)] for step in range(3)]
    halves = (first_half, second_half)
    x_two = [[late_copy(0, side, here, 2 * i) for side in range(2)] for i, here in enumerate(halves)]
    x_alone = [late_copy(1, side, everything, 4) for side in range(2)]
    x_sum = [[late_copy(2, side, here, 6 + 2 * i) for side in range(2)] for i, here in enumerate(halves)]

    add_near(0)
    for side in range(2):
        e_send[side] = total[0, :, early[side]].astype(BF16)
        e[0][side].start()
    for side in range(2):
        add_near(1 + side)
        e_send[2 + side] = total[1 + side, :, early[1 - side]].astype(BF16)
        e[1][side].start()
    for i, here in enumerate(halves):
        add_far(0, i, here)
        for side in range(2):
            x_send[side, here, :] = total[0, here, late[side]].astype(BF16)
            x_two[i][side].start()
    for side in range(2):
        e[0][side].wait_recv()
        e_send[4 + side] = (total[1 + side, :, early[side]] + e_recv[side].astype(F32)).astype(BF16)
        e[2][side].start()
    for side in range(2):
        add_far(1 + side, 2 + side, everything)
        x_send[2 + side] = total[1 + side, :, late[1 - side]].astype(BF16)
        x_alone[side].start()
    for i, here in enumerate(halves):
        for side in range(2):
            x_two[i][side].wait_recv()
            x_send[4 + side, here, :] = (
                total[1 + side, here, late[side]] + x_recv[side, here, :].astype(F32)
            ).astype(BF16)
            x_sum[i][side].start()
    add_near(3)
    add_far(3, 4, everything)
    for side in range(2):
        e[1][side].wait_recv()
        e[2][side].wait_recv()
    for side in range(2):
        out_ref[:, early[side]] = (
            total[3, :, early[side]] + e_recv[4 + side].astype(F32) + e_recv[3 - side].astype(F32)
        )
    for side in range(2):
        x_alone[side].wait_recv()
    for side in range(2):
        total[3, :, late[side]] += x_recv[3 - side].astype(F32)
    for i, here in enumerate(halves):
        for side in range(2):
            x_sum[i][side].wait_recv()
            out_ref[here, late[side]] = total[3, here, late[side]] + x_recv[4 + side, here, :].astype(F32)

    for copy in own_near + near_copies + e[0] + e[1] + e[2] + x_two[0] + x_two[1] + x_alone + x_sum[0] + x_sum[1]:
        copy.wait_send()

    @pl.when(has_r)
    def _():
        for copy in own_r + rel_r_near:
            copy.wait_send()

    @pl.when(has_l)
    def _():
        for copy in own_l + rel_l_near:
            copy.wait_send()

    @pl.when(far_ok)
    def _():
        for copy in own_far + far_copies:
            copy.wait_send()

        @pl.when(has_r)
        def _():
            for copy in rel_r_far:
                copy.wait_send()

        @pl.when(has_l)
        def _():
            for copy in rel_l_far:
                copy.wait_send()


def body(n_slab, n_cross, a_tiles, a_cols, over_tiles, over_rows, over_cols, p_tiles, p_cols):
    rows = CB * TILE // n_cross
    hbm = pl.BlockSpec(memory_space=pl.ANY)
    smem = pl.BlockSpec(memory_space=pltpu.SMEM)
    return pl.pallas_call(
        functools.partial(kernel, n_slab, n_cross),
        out_shape=jax.ShapeDtypeStruct((rows, CW), F32),
        in_specs=[hbm, hbm, hbm, smem, smem, smem, smem],
        out_specs=pl.BlockSpec(memory_space=pltpu.VMEM),
        scratch_shapes=[
            pltpu.VMEM((9, NCH, BROWS, TILE), BF16),
            pltpu.VMEM((18, TILE, WIDE), BF16),
            pltpu.VMEM((NB, K + 1, TILE, TILE), BF16),
            pltpu.VMEM((OV + 1, TILE, TILE), BF16),
            pltpu.VMEM((3, NB * TILE, WIDE), BF16),
            pltpu.VMEM((WIDE, NB * TILE), BF16),
            pltpu.VMEM((NB * TILE, PW), F32),
            pltpu.VMEM((NB * TILE, PW), BF16),
            pltpu.VMEM((n_cross, rows, PW), BF16),
            pltpu.VMEM((n_cross, rows, PW), BF16),
            pltpu.VMEM((n_cross, rows, PW), BF16),
            pltpu.VMEM((n_cross, rows, PW), BF16),
            pltpu.VMEM((n_cross, rows, CW), F32),
            pltpu.VMEM((6, rows, EARLY // 2), BF16),
            pltpu.VMEM((6, rows, EARLY // 2), BF16),
            pltpu.VMEM((6, rows, PW // 2), BF16),
            pltpu.VMEM((6, rows, PW // 2), BF16),
            pltpu.SemaphoreType.DMA((2 + NCH,)),
            pltpu.SemaphoreType.DMA((N_SEMS,)),
            pltpu.SemaphoreType.DMA((N_SEMS,)),
        ],
        compiler_params=pltpu.CompilerParams(collective_id=0, has_side_effects=True),
    )(a_tiles, over_tiles, p_tiles.reshape(NB * KP * TILE, TILE), a_cols, over_rows, over_cols, p_cols)


def solution(mesh):
    return jax.shard_map(
        functools.partial(body, mesh.shape["slab"], mesh.shape["cross"]),
        mesh=mesh,
        in_specs=(
            P(("slab", "cross"), None, None, None),
            P(("slab", "cross"), None),
            P(("slab", "cross"), None, None),
            P(("slab", "cross")),
            P(("slab", "cross")),
            P(("slab", "cross"), None, None, None),
            P(("slab", "cross"), None),
        ),
        out_specs=P(("slab", "cross"), None),
        check_vma=False,
    )
```

time: 43.5 us -> 39.3 us (0.903)
  Pallas kernels: 41.5 us -> 37 us
    pallas_call x1, Pallas kernels: 41.5 us -> 37 us  [body(): pl.pallas_call(functools.partial(kernel, n_slab, n_cross), out_shape=jax....]
where the time goes in v2:
time: 39.3 us; the launch traced here: 38.8 us
  Pallas kernels  37 us (94%)
  local copies, waits for them, and re-layouts  1.82 us (5%)
    pallas_call x1, Pallas kernels, body(): pl.pallas_call(functools.partial(kernel, n_slab, n_cross), out_shape=jax....  37 us
    unnamed x1, local copies, waits for them, and re-layouts  1.82 us

profile of v2, /device:TPU:56, one launch (start us, length us, event | category | flops | bytes accessed | tf_op | source)
XLA Modules:
  0.0 38.8 jit_solution(4026630150133662084)
XLA Ops:
  0.0 37.0 %shard_map.73 = f32[64,1792]{1,0:T(8,128)} custom-call(bf16[2,7,128,128]{3,2,1,0:T(8,128)(2,1)} %a_hbm.1, bf16[4,128,128]{2,1,0:T(8,128)(2,1)} %o_hbm.1, bf16[768,128]{1,0:T(8,128)(2,1)} %bitcast.1, s32[2,7]{1,0:T(2,128)} %a_cols.1, s32[4]{0:T(128)} %over_rows.1, s32[4]{0:T(128)} %over_cols.1, s32[2,3]{1,0:T(2,128)} %p_cols.1), custom_call_target="tpu_custom_call" | custom-call | tf_op jit(solution)/shard_map/pallas_call | solution.py:448
  37.0 1.8 %copy.9 = f32[64,1792]{1,0:T(8,128)} copy(f32[64,1792]{1,0:T(8,128)} %shard_map.73) | data formatting | bytes 917504

commit v3 on v2

v3 whole, which is shorter than its diff:
```python
import functools

import jax
import jax.numpy as jnp
from jax import lax
from jax.experimental import pallas as pl
from jax.experimental.pallas import tpu as pltpu
from jax.sharding import PartitionSpec as P

CB = 2
TILE = 128
NB = 2
KP = 3
K = 7
OV = 4
WIDTH = CB * TILE
WIDE = 3 * WIDTH
PW = 5 * WIDTH
CW = 7 * WIDTH
EARLY = CW - PW
NCH = NB * KP
MARKS = 16
BROWS = MARKS + NCH * TILE
RELAYED = (0, 1, 2, 3)
TURNED = (4, 5)
F32 = jnp.float32
BF16 = jnp.bfloat16

OWN_R, OWN_L, OWN_NEAR, OWN_FAR, REL_L_NEAR, REL_L_FAR, REL_R_NEAR, REL_R_FAR, TURN_R, TURN_L = (
    NCH * i for i in range(10)
)
FAR0 = 10 * NCH
NEAR0 = FAR0 + 9
X0 = NEAR0 + 4
N_SEMS = X0 + 16


def dot(a, b):
    return lax.dot_general(a, b, (((1,), (0,)), ((), ())), preferred_element_type=F32)


def kernel(
    n_slab, n_cross,
    a_hbm, o_hbm, p_hbm, a_cols_hbm, over_rows_hbm, over_cols_hbm, p_cols_hbm,
    out_ref,
    a_cols, over_rows, over_cols, p_cols,
    halo, dense, a_in, o_in, a_dense, p_turned, acc, prod,
    send_far, send_near, recv_far, recv_near, total,
    e_send, e_recv, x_send, x_recv, local_sem, send_sem, recv_sem,
):
    s = lax.axis_index("slab")
    c = lax.axis_index("cross")
    core = lax.rem(s, 2)
    near = s + 1 - 2 * core
    far = s - 1 + 2 * core
    far_ok = jnp.logical_and(far >= 0, far < n_slab)
    right = lax.rem(c + 1, n_cross)
    left = lax.rem(c + n_cross - 1, n_cross)
    has_l = c > 0
    has_r = c < n_cross - 1
    r_near = 2 - 2 * core
    r_far = 2 * core
    rows = CB * TILE // n_cross
    part_rows = rows // 2

    def device(slab, cross):
        return {"slab": slab, "cross": cross}

    def remote(src, dst, i, slab, cross):
        return pltpu.make_async_remote_copy(
            src_ref=src, dst_ref=dst, send_sem=send_sem.at[i], recv_sem=recv_sem.at[i],
            device_id=device(slab, cross), device_id_type=pl.DeviceIdType.MESH,
        )

    barrier = pltpu.get_barrier_semaphore()

    def greet(slab, cross):
        pl.semaphore_signal(
            barrier, inc=1, device_id=device(slab, cross), device_id_type=pl.DeviceIdType.MESH
        )

    @pl.when(far_ok)
    def _():
        greet(far, c)

    greet(s, left)
    greet(s, right)
    greet(near, c)

    load_p = pltpu.make_async_copy(p_hbm, halo.at[4, pl.ds(MARKS, NCH * TILE)], local_sem.at[0])
    load_numbers = pltpu.make_async_copy(p_cols_hbm, p_cols, local_sem.at[1])
    load_a = [
        pltpu.make_async_copy(a_hbm, a_in.at[:, pl.ds(0, K)], local_sem.at[2]),
        pltpu.make_async_copy(a_cols_hbm, a_cols, local_sem.at[3]),
        pltpu.make_async_copy(o_hbm, o_in.at[pl.ds(0, OV)], local_sem.at[4]),
        pltpu.make_async_copy(over_rows_hbm, over_rows, local_sem.at[5]),
        pltpu.make_async_copy(over_cols_hbm, over_cols, local_sem.at[6]),
    ]
    for load in [load_numbers, load_p] + load_a:
        load.start()

    nothing = jnp.full((MARKS, TILE), -1.0, BF16)

    def leave_out(b):
        halo[b, pl.ds(0, MARKS), :] = nothing

    @pl.when(jnp.logical_not(has_l))
    def _():
        for r in range(3):
            leave_out(3 * r)

    @pl.when(jnp.logical_not(has_r))
    def _():
        for r in range(3):
            leave_out(3 * r + 2)

    @pl.when(jnp.logical_not(far_ok))
    def _():
        for u in range(3):
            leave_out(3 * r_far + u)
        recv_far[...] = jnp.zeros_like(recv_far)

    for n in range(NB):
        a_in[n, K] = jnp.zeros((TILE, TILE), BF16)
    o_in[OV] = jnp.zeros((TILE, TILE), BF16)
    acc[...] = jnp.zeros_like(acc)
    total[...] = jnp.zeros_like(total)

    load_numbers.wait()
    row = lax.broadcasted_iota(jnp.int32, (MARKS, TILE), 0)
    value = jnp.full((MARKS, TILE), -1.0, F32)
    for i in range(NCH):
        value = jnp.where(row == i, p_cols[i // KP, i % KP].astype(F32), value)
    halo[4, pl.ds(0, MARKS), :] = value.astype(BF16)
    load_p.wait()
    pl.semaphore_wait(barrier, 3 + far_ok.astype(jnp.int32))

    def halo_copies(b, to, first, slab, cross, chunks=range(NCH)):
        copies = {}
        for h in chunks:
            at = pl.ds(0, MARKS + TILE) if h == 0 else pl.ds(MARKS + h * TILE, TILE)
            copies[h] = remote(halo.at[b, at], halo.at[to, at], first + h, slab, cross)
        return copies

    own_r = halo_copies(4, 3, OWN_R, s, right)
    own_l = halo_copies(4, 5, OWN_L, s, left)
    own_near = halo_copies(4, 3 * r_far + 1, OWN_NEAR, near, c)
    own_far = halo_copies(4, 3 * r_near + 1, OWN_FAR, far, c)
    rel_l_near = halo_copies(3, 3 * r_far, REL_L_NEAR, near, c)
    rel_l_far = halo_copies(3, 3 * r_near, REL_L_FAR, far, c, RELAYED)
    rel_r_near = halo_copies(5, 3 * r_far + 2, REL_R_NEAR, near, c)
    rel_r_far = halo_copies(5, 3 * r_near + 2, REL_R_FAR, far, c, RELAYED)
    turn_r = halo_copies(3 * r_far + 1, 3 * r_far, TURN_R, s, right, TURNED)
    turn_l = halo_copies(3 * r_far + 1, 3 * r_far + 2, TURN_L, s, left, TURNED)

    for h in range(NCH):

        @pl.when(has_r)
        def _():
            own_r[h].start()

        @pl.when(has_l)
        def _():
            own_l[h].start()

    @pl.when(far_ok)
    def _():
        for h in TURNED + RELAYED:
            own_far[h].start()

    for h in range(NCH):
        own_near[h].start()

    def densify(b):
        for n in range(NB):
            tiles, marks = [], []
            numbers = halo[b, pl.ds(0, MARKS), :].astype(F32)
            for i in range(n * KP, n * KP + KP):
                tiles.append(halo[b, pl.ds(MARKS + i * TILE, TILE), :].reshape(8, 16, TILE))
                marks.append(jnp.broadcast_to(numbers[i : i + 1], (16, TILE)).astype(BF16))
            for q in range(3 * CB):
                value = jnp.zeros((8, 16, TILE), BF16)
                for m in range(KP):
                    here = jnp.broadcast_to((marks[m] == jnp.asarray(q, BF16))[None], value.shape)
                    value = jnp.where(here, tiles[m], value)
                dense[2 * b + n, :, pl.ds(q * TILE, TILE)] = value.reshape(TILE, TILE)

    def place_a(r, places=(0, 1)):
        for n in places:
            for t in range(6 * r, 6 * r + 6):
                at = jnp.int32(K)
                for k in range(K):
                    at = jnp.where(a_cols[n, k] == t, k, at)
                value = a_in[n, at].astype(F32)
                for o in range(OV):
                    hit = jnp.logical_and(over_rows[o] == n, over_cols[o] == t)
                    value += o_in[jnp.where(hit, o, OV)].astype(F32)
                a_dense[r, pl.ds(n * TILE, TILE), pl.ds((t % 6) * TILE, TILE)] = value.astype(BF16)

    def relay(h):
        @pl.when(has_l)
        def _():
            own_r[h].wait_recv()
            if h in RELAYED:

                @pl.when(far_ok)
                def _():
                    rel_l_far[h].start()

            rel_l_near[h].start()

        @pl.when(has_r)
        def _():
            own_l[h].wait_recv()
            if h in RELAYED:

                @pl.when(far_ok)
                def _():
                    rel_r_far[h].start()

            rel_r_near[h].start()

    def turn(h):
        @pl.when(far_ok)
        def _():
            own_far[h].wait_recv()

            @pl.when(has_r)
            def _():
                turn_r[h].start()

            @pl.when(has_l)
            def _():
                turn_l[h].start()

    def product_of(r, u, count, j):
        right_side = dense[pl.ds(6 * r + 2 * u, 2 * count), :, pl.ds(j * WIDTH, WIDTH)]
        return dot(
            a_dense[r, :, pl.ds(u * WIDTH, count * WIDTH)], right_side.reshape(count * WIDTH, WIDTH)
        )

    def columns(r, j):
        return pl.ds(pl.multiple_of((r + j) * WIDTH, WIDTH), WIDTH)

    def add_blocks(r, u, count):
        for j in range(3):
            acc[:, columns(r, j)] += product_of(r, u, count, j)

    densify(4)
    for load in load_a:
        load.wait()
    place_a(1, (0,))
    relay(0)
    turn(TURNED[0])
    place_a(1, (1,))
    relay(1)
    turn(TURNED[1])
    for n in range(NB):
        for q in range(3 * CB):
            block = dense[8 + n, :, pl.ds(q * TILE, TILE)]
            p_turned[pl.ds(q * TILE, TILE), pl.ds(n * TILE, TILE)] = block.T
    relay(2)
    place_a(0, (0,))
    relay(3)
    place_a(0, (1,))
    relay(4)
    place_a(2, (0,))
    relay(5)
    place_a(2, (1,))
    densify(3)
    densify(5)
    add_blocks(1, 0, 3)

    for h in range(NCH):
        own_near[h].wait_recv()

    @pl.when(has_l)
    def _():
        for h in range(NCH):
            rel_l_near[h].wait_recv()

    @pl.when(has_r)
    def _():
        for h in range(NCH):
            rel_r_near[h].wait_recv()

    for u in range(3):
        densify(3 * r_near + u)
    add_blocks(r_near, 0, 3)
    for j in range(2):
        at = pl.ds(pl.multiple_of((3 - 3 * core + j) * WIDTH, WIDTH), WIDTH)
        prod[:, at] = acc[:, at].astype(BF16)

    @pl.when(far_ok)
    def _():
        for h in RELAYED:
            own_far[h].wait_recv()

    densify(3 * r_far + 1)
    add_blocks(r_far, 1, 1)

    @pl.when(jnp.logical_and(far_ok, has_l))
    def _():
        for h in RELAYED:
            rel_l_far[h].wait_recv()
        for h in TURNED:
            turn_r[h].wait_recv()

    densify(3 * r_far)

    @pl.when(jnp.logical_and(far_ok, has_r))
    def _():
        for h in RELAYED:
            rel_r_far[h].wait_recv()
        for h in TURNED:
            turn_l[h].wait_recv()

    densify(3 * r_far + 2)
    for j in range(3):
        at = columns(r_far, j)
        prod[:, at] = (acc[:, at] + (product_of(r_far, 0, 1, j) + product_of(r_far, 2, 1, j))).astype(BF16)

    order = [lax.rem(c + off, n_cross) for off in (2, 1, 3, 0)]

    def chunk_of(q, k, at):
        lhs = p_turned[pl.ds(pl.multiple_of(q * WIDTH + order[k] * rows, rows), rows), :]
        return dot(lhs, prod[:, at])

    halves = (pl.ds(0, part_rows), pl.ds(part_rows, part_rows))
    pieces = [(0, b, here) for here in halves for b in range(2)]
    pieces += [(k, b, pl.ds(0, rows)) for k, b in ((1, 1), (2, 0), (1, 0), (2, 1))]
    far_copies = [
        remote(send_far.at[k, b, here], recv_far.at[k, b, here], FAR0 + i, far, c)
        for i, (k, b, here) in enumerate(pieces)
    ]
    far_copies.append(remote(send_far.at[3], recv_far.at[3], FAR0 + 8, far, c))
    near_copies = [remote(send_near.at[k], recv_near.at[k], NEAR0 + k, near, c) for k in range(4)]

    def make_far(k, b):
        send_far[k, b] = chunk_of(r_far, k, pl.ds(b * (PW // 2), PW // 2)).astype(BF16)

    def start_far(*which):
        @pl.when(far_ok)
        def _():
            for i in which:
                far_copies[i].start()

    def send_near_chunk(k):
        for j in range(5):
            at = pl.ds(j * WIDTH, WIDTH)
            send_near[k, :, at] = chunk_of(r_near, k, at).astype(BF16)
        near_copies[k].start()

    def own_chunk(k):
        for j in range(5):
            total[k, :, pl.ds((j + 1) * WIDTH, WIDTH)] = chunk_of(1, k, pl.ds(j * WIDTH, WIDTH))

    make_far(0, 0)
    make_far(0, 1)
    start_far(0, 1, 2, 3)
    send_near_chunk(0)
    make_far(1, 1)
    start_far(4)
    make_far(2, 0)
    start_far(5)
    send_near_chunk(1)
    send_near_chunk(2)
    make_far(1, 0)
    start_far(6)
    make_far(2, 1)
    start_far(7)
    make_far(3, 0)
    make_far(3, 1)
    start_far(8)
    own_chunk(0)
    own_chunk(1)
    own_chunk(2)

    near_at = pl.ds(pl.multiple_of((2 - 2 * core) * WIDTH, WIDTH), PW)
    def add_near(k):
        near_copies[k].wait_recv()
        total[k, :, near_at] += recv_near[k].astype(F32)

    def wait_far(i):
        @pl.when(far_ok)
        def _():
            far_copies[i].wait_recv()

    early_first = pl.multiple_of((5 - 5 * core) * WIDTH, WIDTH)
    late_first = pl.multiple_of(2 * core * WIDTH, WIDTH)
    early = [pl.ds(pl.multiple_of(early_first + i * (EARLY // 2), TILE), EARLY // 2) for i in range(2)]
    late = [pl.ds(pl.multiple_of(late_first + i * (PW // 2), TILE), PW // 2) for i in range(2)]

    to = [right, left]

    def early_copy(step, side):
        i = 2 * step + side
        return remote(e_send.at[i], e_recv.at[i], X0 + i, s, to[side])

    def late_copy(step, side, here, extra):
        i = 2 * step + side
        return remote(x_send.at[i, here], x_recv.at[i, here], X0 + 6 + extra + side, s, to[side])

    e = [[early_copy(step, side) for side in range(2)] for step in range(3)]
    x_two = [[late_copy(0, side, here, 2 * i) for side in range(2)] for i, here in enumerate(halves)]
    x_alone = [late_copy(1, side, pl.ds(0, rows), 4) for side in range(2)]
    x_sum = [[late_copy(2, side, here, 6 + 2 * i) for side in range(2)] for i, here in enumerate(halves)]

    def late_rows(k, b, here):
        return total[k, here, late[b]] + recv_far[k, b, here, :].astype(F32)

    def send_alone(side):
        wait_far(4 + side)
        x_send[2 + side] = late_rows(1 + side, 1 - side, pl.ds(0, rows)).astype(BF16)
        x_alone[side].start()

    add_near(0)
    for side in range(2):
        e_send[side] = total[0, :, early[side]].astype(BF16)
        e[0][side].start()
    for side in range(2):
        add_near(1 + side)
        e_send[2 + side] = total[1 + side, :, early[1 - side]].astype(BF16)
        e[1][side].start()
    for i, here in enumerate(halves):
        for side in range(2):
            wait_far(2 * i + side)
            x_send[side, here, :] = late_rows(0, side, here).astype(BF16)
            x_two[i][side].start()
    send_near_chunk(3)
    own_chunk(3)
    send_alone(0)
    for side in range(2):
        e[0][side].wait_recv()
        e_send[4 + side] = (total[1 + side, :, early[side]] + e_recv[side].astype(F32)).astype(BF16)
        e[2][side].start()
    send_alone(1)
    add_near(3)
    for side in range(2):
        wait_far(6 + side)
        for i, here in enumerate(halves):
            x_two[i][side].wait_recv()
            came = x_recv[side, here, :].astype(F32)
            x_send[4 + side, here, :] = (late_rows(1 + side, side, here) + came).astype(BF16)
            x_sum[i][side].start()
    for side in range(2):
        e[1][side].wait_recv()
        e[2][side].wait_recv()
    for side in range(2):
        out_ref[:, early[side]] = (
            total[3, :, early[side]] + e_recv[4 + side].astype(F32) + e_recv[3 - side].astype(F32)
        )
    wait_far(8)
    for side in range(2):
        x_alone[side].wait_recv()
    for side in range(2):
        total[3, :, late[side]] = late_rows(3, side, pl.ds(0, rows)) + x_recv[3 - side].astype(F32)
    for side in range(2):
        for i, here in enumerate(halves):
            x_sum[i][side].wait_recv()
            out_ref[here, late[side]] = total[3, here, late[side]] + x_recv[4 + side, here, :].astype(F32)

    for copy in list(own_near.values()) + near_copies + e[0] + e[1] + e[2] + x_two[0] + x_two[1] + x_alone + x_sum[0] + x_sum[1]:
        copy.wait_send()

    @pl.when(has_r)
    def _():
        for copy in list(own_r.values()) + list(rel_r_near.values()):
            copy.wait_send()

    @pl.when(has_l)
    def _():
        for copy in list(own_l.values()) + list(rel_l_near.values()):
            copy.wait_send()

    @pl.when(far_ok)
    def _():
        for copy in list(own_far.values()) + far_copies:
            copy.wait_send()

        @pl.when(has_r)
        def _():
            for copy in list(rel_r_far.values()) + list(turn_r.values()):
                copy.wait_send()

        @pl.when(has_l)
        def _():
            for copy in list(rel_l_far.values()) + list(turn_l.values()):
                copy.wait_send()


def body(n_slab, n_cross, a_tiles, a_cols, over_tiles, over_rows, over_cols, p_tiles, p_cols):
    rows = CB * TILE // n_cross
    hbm = pl.BlockSpec(memory_space=pl.ANY)
    return pl.pallas_call(
        functools.partial(kernel, n_slab, n_cross),
        out_shape=pltpu.VMEM((rows, CW), F32),
        in_specs=[hbm] * 7,
        out_specs=pl.BlockSpec(memory_space=pltpu.VMEM),
        scratch_shapes=[
            pltpu.SMEM((NB, K), jnp.int32),
            pltpu.SMEM((OV,), jnp.int32),
            pltpu.SMEM((OV,), jnp.int32),
            pltpu.SMEM((NB, KP), jnp.int32),
            pltpu.VMEM((9, BROWS, TILE), BF16),
            pltpu.VMEM((18, TILE, WIDE), BF16),
            pltpu.VMEM((NB, K + 1, TILE, TILE), BF16),
            pltpu.VMEM((OV + 1, TILE, TILE), BF16),
            pltpu.VMEM((3, NB * TILE, WIDE), BF16),
            pltpu.VMEM((WIDE, NB * TILE), BF16),
            pltpu.VMEM((NB * TILE, PW), F32),
            pltpu.VMEM((NB * TILE, PW), BF16),
            pltpu.VMEM((n_cross, 2, rows, PW // 2), BF16),
            pltpu.VMEM((n_cross, rows, PW), BF16),
            pltpu.VMEM((n_cross, 2, rows, PW // 2), BF16),
            pltpu.VMEM((n_cross, rows, PW), BF16),
            pltpu.VMEM((n_cross, rows, CW), F32),
            pltpu.VMEM((6, rows, EARLY // 2), BF16),
            pltpu.VMEM((6, rows, EARLY // 2), BF16),
            pltpu.VMEM((6, rows, PW // 2), BF16),
            pltpu.VMEM((6, rows, PW // 2), BF16),
            pltpu.SemaphoreType.DMA((7,)),
            pltpu.SemaphoreType.DMA((N_SEMS,)),
            pltpu.SemaphoreType.DMA((N_SEMS,)),
        ],
        compiler_params=pltpu.CompilerParams(collective_id=0, has_side_effects=True),
    )(a_tiles, over_tiles, p_tiles.reshape(NB * KP * TILE, TILE), a_cols, over_rows, over_cols, p_cols)


def solution(mesh):
    return jax.shard_map(
        functools.partial(body, mesh.shape["slab"], mesh.shape["cross"]),
        mesh=mesh,
        in_specs=(
            P(("slab", "cross"), None, None, None),
            P(("slab", "cross"), None),
            P(("slab", "cross"), None, None),
            P(("slab", "cross")),
            P(("slab", "cross")),
            P(("slab", "cross"), None, None, None),
            P(("slab", "cross"), None),
        ),
        out_specs=P(("slab", "cross"), None),
        check_vma=False,
    )
```

time: 39.3 us -> 35.5 us (0.903)
  Pallas kernels: 37 us -> 34.6 us
  local copies, waits for them, and re-layouts: 1.82 us -> 0.77 us
    pallas_call x1, Pallas kernels: 37 us -> 34.6 us  [body(): pl.pallas_call(functools.partial(kernel, n_slab, n_cross), out_shape=pltp...]
    unnamed x1, local copies, waits for them, and re-layouts: 1.82 us -> 0.77 us
where the time goes in v3:
time: 35.5 us; the launch traced here: 35.3 us
  Pallas kernels  34.6 us (97%)
  local copies, waits for them, and re-layouts  0.77 us (2%)
    pallas_call x1, Pallas kernels, body(): pl.pallas_call(functools.partial(kernel, n_slab, n_cross), out_shape=pltp...  34.6 us
    unnamed x1, local copies, waits for them, and re-layouts  0.77 us

profile of v3, /device:TPU:56, one launch (start us, length us, event | category | flops | bytes accessed | tf_op | source)
XLA Modules:
  0.0 35.3 jit_solution(1487745580477876917)
XLA Ops:
  0.0 34.6 %shard_map.73 = f32[64,1792]{1,0:T(8,128)S(1)} custom-call(bf16[2,7,128,128]{3,2,1,0:T(8,128)(2,1)} %a_hbm.1, bf16[4,128,128]{2,1,0:T(8,128)(2,1)} %o_hbm.1, bf16[768,128]{1,0:T(8,128)(2,1)} %bitcast.1, s32[2,7]{1,0:T(2,128)} %a_cols_hbm.1, s32[4]{0:T(128)} %over_rows_hbm.1, s32[4]{0:T(128)} %over_cols_hbm.1, s32[2,3]{1,0:T(2,128)} %p_cols_hbm.1), custom_call_target="tpu_custom_call" | custom-call | tf_op jit(solution)/shard_map/pallas_call | solution.py:495
  34.6 0.8 %copy.9 = f32[64,1792]{1,0:T(8,128)} copy(f32[64,1792]{1,0:T(8,128)S(1)} %shard_map.73) | data formatting | bytes 917504

commit v4 on v3

--- a/solution.py
+++ b/solution.py
@@ -17,7 +17,7 @@
 WIDE = 3 * WIDTH
 PW = 5 * WIDTH
 CW = 7 * WIDTH
-EARLY = CW - PW
+EARLY = PW - WIDE
 NCH = NB * KP
 MARKS = 16
 BROWS = MARKS + NCH * TILE
@@ -30,9 +30,11 @@
     NCH * i for i in range(10)
 )
 FAR0 = 10 * NCH
-NEAR0 = FAR0 + 9
-X0 = NEAR0 + 4
-N_SEMS = X0 + 16
+FAR_EARLY = FAR0 + 9
+NEAR0 = FAR_EARLY + 4
+NEAR_EARLY = NEAR0 + 4
+X0 = NEAR_EARLY + 1
+N_SEMS = X0 + 22
 
 
 def dot(a, b):
@@ -45,6 +47,7 @@
     out_ref,
     a_cols, over_rows, over_cols, p_cols,
     halo, dense, a_in, o_in, a_dense, p_turned, acc, prod,
+    early_far, early_near, got_early_far, got_early_near,
     send_far, send_near, recv_far, recv_near, total,
     e_send, e_recv, x_send, x_recv, local_sem, send_sem, recv_sem,
 ):
@@ -119,12 +122,7 @@
         for u in range(3):
             leave_out(3 * r_far + u)
         recv_far[...] = jnp.zeros_like(recv_far)
-
-    for n in range(NB):
-        a_in[n, K] = jnp.zeros((TILE, TILE), BF16)
-    o_in[OV] = jnp.zeros((TILE, TILE), BF16)
-    acc[...] = jnp.zeros_like(acc)
-    total[...] = jnp.zeros_like(total)
+        got_early_far[...] = jnp.zeros_like(got_early_far)
 
     load_numbers.wait()
     row = lax.broadcasted_iota(jnp.int32, (MARKS, TILE), 0)
@@ -171,8 +169,14 @@
     for h in range(NCH):
         own_near[h].start()
 
-    def densify(b):
-        for n in range(NB):
+    for n in range(NB):
+        a_in[n, K] = jnp.zeros((TILE, TILE), BF16)
+    o_in[OV] = jnp.zeros((TILE, TILE), BF16)
+    acc[...] = jnp.zeros_like(acc)
+    total[...] = jnp.zeros_like(total)
+
+    def densify(b, places=(0, 1)):
+        for n in places:
             tiles, marks = [], []
             numbers = halo[b, pl.ds(0, MARKS), :].astype(F32)
             for i in range(n * KP, n * KP + KP):
@@ -287,9 +291,33 @@
     for u in range(3):
         densify(3 * r_near + u)
     add_blocks(r_near, 0, 3)
+    order = [lax.rem(c + off, n_cross) for off in (2, 1, 3, 0)]
+    early_at = (3 - 3 * core) * WIDTH
+    late_at = 2 * core * WIDTH
+
+    def chunk_of(q, k, first, width):
+        lhs = p_turned[pl.ds(pl.multiple_of(q * WIDTH + order[k] * rows, rows), rows), :]
+        return dot(lhs, prod[:, pl.ds(pl.multiple_of(first, TILE), width)])
+
     for j in range(2):
-        at = pl.ds(pl.multiple_of((3 - 3 * core + j) * WIDTH, WIDTH), WIDTH)
+        at = pl.ds(pl.multiple_of(early_at + j * WIDTH, WIDTH), WIDTH)
         prod[:, at] = acc[:, at].astype(BF16)
+
+    early_far_copies = [remote(early_far.at[k], got_early_far.at[k], FAR_EARLY + k, far, c) for k in range(4)]
+    early_near_copy = remote(early_near, got_early_near, NEAR_EARLY, near, c)
+    for k in range(4):
+        early_far[k] = chunk_of(r_far, k, early_at, EARLY).astype(BF16)
+
+        @pl.when(far_ok)
+        def _():
+            early_far_copies[k].start()
+
+    for k in range(4):
+        early_near[k] = chunk_of(r_near, k, early_at, EARLY).astype(BF16)
+    early_near_copy.start()
+    for k in range(4):
+        at = pl.ds(pl.multiple_of(early_at + WIDTH, WIDTH), EARLY)
+        total[k, :, at] = chunk_of(1, k, early_at, EARLY)
 
     @pl.when(far_ok)
     def _():
@@ -299,36 +327,34 @@
     densify(3 * r_far + 1)
     add_blocks(r_far, 1, 1)
 
-    @pl.when(jnp.logical_and(far_ok, has_l))
-    def _():
-        for h in RELAYED:
-            rel_l_far[h].wait_recv()
-        for h in TURNED:
-            turn_r[h].wait_recv()
-
-    densify(3 * r_far)
-
-    @pl.when(jnp.logical_and(far_ok, has_r))
-    def _():
-        for h in RELAYED:
-            rel_r_far[h].wait_recv()
-        for h in TURNED:
-            turn_l[h].wait_recv()
-
-    densify(3 * r_far + 2)
+    first, last = RELAYED[:KP], RELAYED[KP:]
+    diagonal = ((0, has_l, rel_l_far, turn_r), (2, has_r, rel_r_far, turn_l))
+    for u, has, relayed, turned in diagonal:
+
+        @pl.when(jnp.logical_and(far_ok, has))
+        def _():
+            for h in first:
+                relayed[h].wait_recv()
+
+        densify(3 * r_far + u, (0,))
+    for u, has, relayed, turned in diagonal:
+
+        @pl.when(jnp.logical_and(far_ok, has))
+        def _():
+            for h in last:
+                relayed[h].wait_recv()
+            for h in TURNED:
+                turned[h].wait_recv()
+
+        densify(3 * r_far + u, (1,))
     for j in range(3):
         at = columns(r_far, j)
         prod[:, at] = (acc[:, at] + (product_of(r_far, 0, 1, j) + product_of(r_far, 2, 1, j))).astype(BF16)
 
-    order = [lax.rem(c + off, n_cross) for off in (2, 1, 3, 0)]
-
-    def chunk_of(q, k, at):
-        lhs = p_turned[pl.ds(pl.multiple_of(q * WIDTH + order[k] * rows, rows), rows), :]
-        return dot(lhs, prod[:, at])
-
     halves = (pl.ds(0, part_rows), pl.ds(part_rows, part_rows))
+    every = pl.ds(0, rows)
     pieces = [(0, b, here) for here in halves for b in range(2)]
-    pieces += [(k, b, pl.ds(0, rows)) for k, b in ((1, 1), (2, 0), (1, 0), (2, 1))]
+    pieces += [(k, b, every) for k, b in ((1, 1), (2, 0), (1, 0), (2, 1))]
     far_copies = [
         remote(send_far.at[k, b, here], recv_far.at[k, b, here], FAR0 + i, far, c)
         for i, (k, b, here) in enumerate(pieces)
@@ -336,8 +362,10 @@
     far_copies.append(remote(send_far.at[3], recv_far.at[3], FAR0 + 8, far, c))
     near_copies = [remote(send_near.at[k], recv_near.at[k], NEAR0 + k, near, c) for k in range(4)]
 
-    def make_far(k, b):
-        send_far[k, b] = chunk_of(r_far, k, pl.ds(b * (PW // 2), PW // 2)).astype(BF16)
+    def make_far(k):
+        value = chunk_of(r_far, k, late_at, WIDE).astype(BF16)
+        for b in range(2):
+            send_far[k, b] = value[:, b * (WIDE // 2) : (b + 1) * (WIDE // 2)]
 
     def start_far(*which):
         @pl.when(far_ok)
@@ -345,122 +373,145 @@
             for i in which:
                 far_copies[i].start()
 
-    def send_near_chunk(k):
-        for j in range(5):
-            at = pl.ds(j * WIDTH, WIDTH)
-            send_near[k, :, at] = chunk_of(r_near, k, at).astype(BF16)
+    def make_near(k):
+        send_near[k] = chunk_of(r_near, k, late_at, WIDE).astype(BF16)
         near_copies[k].start()
 
-    def own_chunk(k):
-        for j in range(5):
-            total[k, :, pl.ds((j + 1) * WIDTH, WIDTH)] = chunk_of(1, k, pl.ds(j * WIDTH, WIDTH))
-
-    make_far(0, 0)
-    make_far(0, 1)
-    start_far(0, 1, 2, 3)
-    send_near_chunk(0)
-    make_far(1, 1)
-    start_far(4)
-    make_far(2, 0)
-    start_far(5)
-    send_near_chunk(1)
-    send_near_chunk(2)
-    make_far(1, 0)
-    start_far(6)
-    make_far(2, 1)
-    start_far(7)
-    make_far(3, 0)
-    make_far(3, 1)
-    start_far(8)
-    own_chunk(0)
-    own_chunk(1)
-    own_chunk(2)
-
-    near_at = pl.ds(pl.multiple_of((2 - 2 * core) * WIDTH, WIDTH), PW)
+    def make_own(k):
+        at = pl.ds(pl.multiple_of(late_at + WIDTH, WIDTH), WIDE)
+        total[k, :, at] = chunk_of(1, k, late_at, WIDE)
+
+    near_first = 2 * (1 - core) * WIDTH
+    near_early = pl.ds(pl.multiple_of(near_first + 3 * core * WIDTH, WIDTH), EARLY)
+    near_late = pl.ds(pl.multiple_of(near_first + 2 * (1 - core) * WIDTH, WIDTH), WIDE)
+
     def add_near(k):
+        total[k, :, near_early] += got_early_near[k].astype(F32)
         near_copies[k].wait_recv()
-        total[k, :, near_at] += recv_near[k].astype(F32)
+        total[k, :, near_late] += recv_near[k].astype(F32)
 
     def wait_far(i):
         @pl.when(far_ok)
         def _():
             far_copies[i].wait_recv()
 
-    early_first = pl.multiple_of((5 - 5 * core) * WIDTH, WIDTH)
-    late_first = pl.multiple_of(2 * core * WIDTH, WIDTH)
-    early = [pl.ds(pl.multiple_of(early_first + i * (EARLY // 2), TILE), EARLY // 2) for i in range(2)]
-    late = [pl.ds(pl.multiple_of(late_first + i * (PW // 2), TILE), PW // 2) for i in range(2)]
+    starts = (5 * core * WIDTH, 5 * (1 - core) * WIDTH, 2 * WIDTH)
+    widths = (EARLY // 2, EARLY // 2, WIDE // 2)
+    group = [
+        [pl.ds(pl.multiple_of(start + b * width, TILE), width) for b in range(2)]
+        for start, width in zip(starts, widths)
+    ]
 
     to = [right, left]
 
-    def early_copy(step, side):
+    def small_copy(g, step, side):
+        i = 6 * g + 2 * step + side
+        return remote(e_send.at[i], e_recv.at[i], X0 + i, s, to[side])
+
+    def late_copy(step, side, here, number):
         i = 2 * step + side
-        return remote(e_send.at[i], e_recv.at[i], X0 + i, s, to[side])
-
-    def late_copy(step, side, here, extra):
-        i = 2 * step + side
-        return remote(x_send.at[i, here], x_recv.at[i, here], X0 + 6 + extra + side, s, to[side])
-
-    e = [[early_copy(step, side) for side in range(2)] for step in range(3)]
+        return remote(x_send.at[i, here], x_recv.at[i, here], X0 + 12 + number + side, s, to[side])
+
+    small = [[[small_copy(g, step, side) for side in range(2)] for step in range(3)] for g in range(2)]
     x_two = [[late_copy(0, side, here, 2 * i) for side in range(2)] for i, here in enumerate(halves)]
-    x_alone = [late_copy(1, side, pl.ds(0, rows), 4) for side in range(2)]
+    x_alone = [late_copy(1, side, every, 4) for side in range(2)]
     x_sum = [[late_copy(2, side, here, 6 + 2 * i) for side in range(2)] for i, here in enumerate(halves)]
 
+    def small_rows(g, k, b):
+        value = total[k, :, group[g][b]]
+        if g == 0:
+            value += got_early_far[k, :, b * widths[0] : (b + 1) * widths[0]].astype(F32)
+        return value
+
+    def send_small(g, step, side):
+        k = (0, 1 + side, 1 + side)[step]
+        b = (side, 1 - side, side)[step]
+        value = small_rows(g, k, b)
+        if step == 2:
+            small[g][0][side].wait_recv()
+            value += e_recv[6 * g + side].astype(F32)
+        e_send[6 * g + 2 * step + side] = value.astype(BF16)
+        small[g][step][side].start()
+
     def late_rows(k, b, here):
-        return total[k, here, late[b]] + recv_far[k, b, here, :].astype(F32)
+        return total[k, here, group[2][b]] + recv_far[k, b, here, :].astype(F32)
 
     def send_alone(side):
         wait_far(4 + side)
-        x_send[2 + side] = late_rows(1 + side, 1 - side, pl.ds(0, rows)).astype(BF16)
+        x_send[2 + side] = late_rows(1 + side, 1 - side, every).astype(BF16)
         x_alone[side].start()
 
+    make_far(0)
+    start_far(0, 1, 2, 3)
+    make_own(0)
+
+    @pl.when(far_ok)
+    def _():
+        for copy in early_far_copies:
+            copy.wait_recv()
+
+    for side in range(2):
+        send_small(0, 0, side)
+    make_near(0)
+    for k in (1, 2):
+        make_far(k)
+        start_far(3 + k)
+        make_own(k)
+        send_small(0, 1, k - 1)
+        make_near(k)
+    start_far(6, 7)
+    early_near_copy.wait_recv()
     add_near(0)
     for side in range(2):
-        e_send[side] = total[0, :, early[side]].astype(BF16)
-        e[0][side].start()
+        send_small(1, 0, side)
     for side in range(2):
         add_near(1 + side)
-        e_send[2 + side] = total[1 + side, :, early[1 - side]].astype(BF16)
-        e[1][side].start()
+        send_small(1, 1, side)
+    make_far(3)
+    start_far(8)
     for i, here in enumerate(halves):
         for side in range(2):
             wait_far(2 * i + side)
             x_send[side, here, :] = late_rows(0, side, here).astype(BF16)
             x_two[i][side].start()
-    send_near_chunk(3)
-    own_chunk(3)
-    send_alone(0)
-    for side in range(2):
-        e[0][side].wait_recv()
-        e_send[4 + side] = (total[1 + side, :, early[side]] + e_recv[side].astype(F32)).astype(BF16)
-        e[2][side].start()
-    send_alone(1)
-    add_near(3)
+    make_near(3)
+    make_own(3)
+    for side in range(2):
+        send_small(0, 2, side)
+    for side in range(2):
+        send_alone(side)
+    for side in range(2):
+        send_small(1, 2, side)
     for side in range(2):
         wait_far(6 + side)
-        for i, here in enumerate(halves):
+    for i, here in enumerate(halves):
+        for side in range(2):
             x_two[i][side].wait_recv()
             came = x_recv[side, here, :].astype(F32)
             x_send[4 + side, here, :] = (late_rows(1 + side, side, here) + came).astype(BF16)
             x_sum[i][side].start()
-    for side in range(2):
-        e[1][side].wait_recv()
-        e[2][side].wait_recv()
-    for side in range(2):
-        out_ref[:, early[side]] = (
-            total[3, :, early[side]] + e_recv[4 + side].astype(F32) + e_recv[3 - side].astype(F32)
-        )
+    add_near(3)
+    for g in range(2):
+        for step in (1, 2):
+            for side in range(2):
+                small[g][step][side].wait_recv()
+        for side in range(2):
+            out_ref[:, group[g][side]] = (
+                small_rows(g, 3, side) + e_recv[6 * g + 4 + side].astype(F32) + e_recv[6 * g + 3 - side].astype(F32)
+            )
     wait_far(8)
     for side in range(2):
         x_alone[side].wait_recv()
     for side in range(2):
-        total[3, :, late[side]] = late_rows(3, side, pl.ds(0, rows)) + x_recv[3 - side].astype(F32)
-    for side in range(2):
-        for i, here in enumerate(halves):
+        total[3, :, group[2][side]] = late_rows(3, side, every) + x_recv[3 - side].astype(F32)
+    for i, here in enumerate(halves):
+        for side in range(2):
             x_sum[i][side].wait_recv()
-            out_ref[here, late[side]] = total[3, here, late[side]] + x_recv[4 + side, here, :].astype(F32)
-
-    for copy in list(own_near.values()) + near_copies + e[0] + e[1] + e[2] + x_two[0] + x_two[1] + x_alone + x_sum[0] + x_sum[1]:
+            out_ref[here, group[2][side]] = total[3, here, group[2][side]] + x_recv[4 + side, here, :].astype(F32)
+
+    sums = [copy for steps in small for sides in steps for copy in sides]
+    sums += x_two[0] + x_two[1] + x_alone + x_sum[0] + x_sum[1]
+    for copy in list(own_near.values()) + [early_near_copy] + near_copies + sums:
         copy.wait_send()
 
     @pl.when(has_r)
@@ -475,7 +526,7 @@
 
     @pl.when(far_ok)
     def _():
-        for copy in list(own_far.values()) + far_copies:
+        for copy in list(own_far.values()) + early_far_copies + far_copies:
             copy.wait_send()
 
         @pl.when(has_r)
@@ -510,15 +561,19 @@
             pltpu.VMEM((WIDE, NB * TILE), BF16),
             pltpu.VMEM((NB * TILE, PW), F32),
             pltpu.VMEM((NB * TILE, PW), BF16),
-            pltpu.VMEM((n_cross, 2, rows, PW // 2), BF16),
-            pltpu.VMEM((n_cross, rows, PW), BF16),
-            pltpu.VMEM((n_cross, 2, rows, PW // 2), BF16),
-            pltpu.VMEM((n_cross, rows, PW), BF16),
+            pltpu.VMEM((n_cross, rows, EARLY), BF16),
+            pltpu.VMEM((n_cross, rows, EARLY), BF16),
+            pltpu.VMEM((n_cross, rows, EARLY), BF16),
+            pltpu.VMEM((n_cross, rows, EARLY), BF16),
+            pltpu.VMEM((n_cross, 2, rows, WIDE // 2), BF16),
+            pltpu.VMEM((n_cross, rows, WIDE), BF16),
+            pltpu.VMEM((n_cross, 2, rows, WIDE // 2), BF16),
+            pltpu.VMEM((n_cross, rows, WIDE), BF16),
             pltpu.VMEM((n_cross, rows, CW), F32),
-            pltpu.VMEM((6, rows, EARLY // 2), BF16),
-            pltpu.VMEM((6, rows, EARLY // 2), BF16),
-            pltpu.VMEM((6, rows, PW // 2), BF16),
-            pltpu.VMEM((6, rows, PW // 2), BF16),
+            pltpu.VMEM((12, rows, EARLY // 2), BF16),
+            pltpu.VMEM((12, rows, EARLY // 2), BF16),
+            pltpu.VMEM((6, rows, WIDE // 2), BF16),
+            pltpu.VMEM((6, rows, WIDE // 2), BF16),
             pltpu.SemaphoreType.DMA((7,)),
             pltpu.SemaphoreType.DMA((N_SEMS,)),
             pltpu.SemaphoreType.DMA((N_SEMS,)),

time: 35.5 us -> 38.6 us (1.087)
  Pallas kernels: 34.6 us -> 37.4 us
    pallas_call x1, Pallas kernels: 34.6 us -> 37.4 us  [body(): pl.pallas_call(functools.partial(kernel, n_slab, n_cross), out_shape=pltp...]
where the time goes in v4:
time: 38.6 us; the launch traced here: 38.2 us
  Pallas kernels  37.4 us (97%)
  local copies, waits for them, and re-layouts  0.77 us (2%)
    pallas_call x1, Pallas kernels, body(): pl.pallas_call(functools.partial(kernel, n_slab, n_cross), out_shape=pltp...  37.4 us

profile of v4, /device:TPU:56, one launch (start us, length us, event | category | flops | bytes accessed | tf_op | source)
XLA Modules:
  0.0 38.2 jit_solution(11211787743468337370)
XLA Ops:
  0.0 37.4 %shard_map.73 = f32[64,1792]{1,0:T(8,128)S(1)} custom-call(bf16[2,7,128,128]{3,2,1,0:T(8,128)(2,1)} %a_hbm.1, bf16[4,128,128]{2,1,0:T(8,128)(2,1)} %o_hbm.1, bf16[768,128]{1,0:T(8,128)(2,1)} %bitcast.1, s32[2,7]{1,0:T(2,128)} %a_cols_hbm.1, s32[4]{0:T(128)} %over_rows_hbm.1, s32[4]{0:T(128)} %over_cols_hbm.1, s32[2,3]{1,0:T(2,128)} %p_cols_hbm.1), custom_call_target="tpu_custom_call" | custom-call | tf_op jit(solution)/shard_map/pallas_call | solution.py:546
  37.4 0.8 %copy.9 = f32[64,1792]{1,0:T(8,128)} copy(f32[64,1792]{1,0:T(8,128)S(1)} %shard_map.73) | data formatting | bytes 917504

commit v5 on v3

--- a/solution.py
+++ b/solution.py
@@ -30,7 +30,8 @@
     NCH * i for i in range(10)
 )
 FAR0 = 10 * NCH
-NEAR0 = FAR0 + 9
+BESIDE = FAR0 + 7
+NEAR0 = BESIDE + 2
 X0 = NEAR0 + 4
 N_SEMS = X0 + 16
 
@@ -45,7 +46,7 @@
     out_ref,
     a_cols, over_rows, over_cols, p_cols,
     halo, dense, a_in, o_in, a_dense, p_turned, acc, prod,
-    send_far, send_near, recv_far, recv_near, total,
+    send_far, send_near, recv_far, recv_near, last_far, beside, total,
     e_send, e_recv, x_send, x_recv, local_sem, send_sem, recv_sem,
 ):
     s = lax.axis_index("slab")
@@ -120,12 +121,6 @@
             leave_out(3 * r_far + u)
         recv_far[...] = jnp.zeros_like(recv_far)
 
-    for n in range(NB):
-        a_in[n, K] = jnp.zeros((TILE, TILE), BF16)
-    o_in[OV] = jnp.zeros((TILE, TILE), BF16)
-    acc[...] = jnp.zeros_like(acc)
-    total[...] = jnp.zeros_like(total)
-
     load_numbers.wait()
     row = lax.broadcasted_iota(jnp.int32, (MARKS, TILE), 0)
     value = jnp.full((MARKS, TILE), -1.0, F32)
@@ -171,8 +166,14 @@
     for h in range(NCH):
         own_near[h].start()
 
-    def densify(b):
-        for n in range(NB):
+    for n in range(NB):
+        a_in[n, K] = jnp.zeros((TILE, TILE), BF16)
+    o_in[OV] = jnp.zeros((TILE, TILE), BF16)
+    acc[...] = jnp.zeros_like(acc)
+    total[...] = jnp.zeros_like(total)
+
+    def densify(b, places=(0, 1)):
+        for n in places:
             tiles, marks = [], []
             numbers = halo[b, pl.ds(0, MARKS), :].astype(F32)
             for i in range(n * KP, n * KP + KP):
@@ -242,80 +243,81 @@
     def columns(r, j):
         return pl.ds(pl.multiple_of((r + j) * WIDTH, WIDTH), WIDTH)
 
-    def add_blocks(r, u, count):
+    def add_own(r):
+        densify(3 * r + 1)
         for j in range(3):
-            acc[:, columns(r, j)] += product_of(r, u, count, j)
-
-    densify(4)
+            acc[:, columns(r, j)] += product_of(r, 1, 1, j)
+
+    def add_sides(r):
+        for j in range(3):
+            acc[:, columns(r, j)] += product_of(r, 0, 1, j) + product_of(r, 2, 1, j)
+
+    near_sides = ((0, has_l, rel_l_near), (2, has_r, rel_r_near))
+    far_sides = ((0, has_l, rel_l_far, turn_r), (2, has_r, rel_r_far, turn_l))
+    first, rest = range(KP), range(KP, NCH)
+
+    def near_rows(n):
+        for u, has, relayed in near_sides:
+
+            @pl.when(has)
+            def _():
+                for h in (first, rest)[n]:
+                    relayed[h].wait_recv()
+
+            densify(3 * r_near + u, (n,))
+
+    def far_rows(n):
+        for u, has, relayed, turned in far_sides:
+
+            @pl.when(jnp.logical_and(far_ok, has))
+            def _():
+                for h in (first, rest)[n]:
+                    (relayed if h in RELAYED else turned)[h].wait_recv()
+
+            densify(3 * r_far + u, (n,))
+
     for load in load_a:
         load.wait()
-    place_a(1, (0,))
+    place_a(1)
     relay(0)
     turn(TURNED[0])
-    place_a(1, (1,))
+    add_own(1)
     relay(1)
     turn(TURNED[1])
     for n in range(NB):
         for q in range(3 * CB):
             block = dense[8 + n, :, pl.ds(q * TILE, TILE)]
             p_turned[pl.ds(q * TILE, TILE), pl.ds(n * TILE, TILE)] = block.T
+    place_a(0)
     relay(2)
-    place_a(0, (0,))
+    place_a(2)
     relay(3)
-    place_a(0, (1,))
-    relay(4)
-    place_a(2, (0,))
-    relay(5)
-    place_a(2, (1,))
-    densify(3)
-    densify(5)
-    add_blocks(1, 0, 3)
-
+    densify(3, (0,))
+    densify(5, (0,))
     for h in range(NCH):
         own_near[h].wait_recv()
-
-    @pl.when(has_l)
-    def _():
-        for h in range(NCH):
-            rel_l_near[h].wait_recv()
-
-    @pl.when(has_r)
-    def _():
-        for h in range(NCH):
-            rel_r_near[h].wait_recv()
-
-    for u in range(3):
-        densify(3 * r_near + u)
-    add_blocks(r_near, 0, 3)
+    add_own(r_near)
+    relay(4)
+    near_rows(0)
+
+    @pl.when(far_ok)
+    def _():
+        for h in RELAYED:
+            own_far[h].wait_recv()
+
+    relay(5)
+    add_own(r_far)
+    densify(3, (1,))
+    densify(5, (1,))
+    add_sides(1)
+    near_rows(1)
+    add_sides(r_near)
     for j in range(2):
         at = pl.ds(pl.multiple_of((3 - 3 * core + j) * WIDTH, WIDTH), WIDTH)
         prod[:, at] = acc[:, at].astype(BF16)
 
-    @pl.when(far_ok)
-    def _():
-        for h in RELAYED:
-            own_far[h].wait_recv()
-
-    densify(3 * r_far + 1)
-    add_blocks(r_far, 1, 1)
-
-    @pl.when(jnp.logical_and(far_ok, has_l))
-    def _():
-        for h in RELAYED:
-            rel_l_far[h].wait_recv()
-        for h in TURNED:
-            turn_r[h].wait_recv()
-
-    densify(3 * r_far)
-
-    @pl.when(jnp.logical_and(far_ok, has_r))
-    def _():
-        for h in RELAYED:
-            rel_r_far[h].wait_recv()
-        for h in TURNED:
-            turn_l[h].wait_recv()
-
-    densify(3 * r_far + 2)
+    far_rows(0)
+    far_rows(1)
     for j in range(3):
         at = columns(r_far, j)
         prod[:, at] = (acc[:, at] + (product_of(r_far, 0, 1, j) + product_of(r_far, 2, 1, j))).astype(BF16)
@@ -328,12 +330,16 @@
 
     halves = (pl.ds(0, part_rows), pl.ds(part_rows, part_rows))
     pieces = [(0, b, here) for here in halves for b in range(2)]
-    pieces += [(k, b, pl.ds(0, rows)) for k, b in ((1, 1), (2, 0), (1, 0), (2, 1))]
+    pieces += [(k, b, pl.ds(0, rows)) for k, b in ((1, 0), (2, 1))]
     far_copies = [
         remote(send_far.at[k, b, here], recv_far.at[k, b, here], FAR0 + i, far, c)
         for i, (k, b, here) in enumerate(pieces)
     ]
-    far_copies.append(remote(send_far.at[3], recv_far.at[3], FAR0 + 8, far, c))
+    far_copies.append(remote(send_far.at[3], recv_far.at[3], FAR0 + 6, far, c))
+    beside_copies = [
+        remote(send_far.at[1 + side, 1 - side], beside.at[1 - side], BESIDE + side, s, (right, left)[side])
+        for side in range(2)
+    ]
     near_copies = [remote(send_near.at[k], recv_near.at[k], NEAR0 + k, near, c) for k in range(4)]
 
     def make_far(k, b):
@@ -358,20 +364,19 @@
     make_far(0, 0)
     make_far(0, 1)
     start_far(0, 1, 2, 3)
+    for side in range(2):
+        make_far(1 + side, 1 - side)
+
+        @pl.when(far_ok)
+        def _():
+            beside_copies[side].start()
+
     send_near_chunk(0)
-    make_far(1, 1)
-    start_far(4)
-    make_far(2, 0)
-    start_far(5)
+    for side in range(2):
+        make_far(1 + side, side)
+        start_far(4 + side)
     send_near_chunk(1)
     send_near_chunk(2)
-    make_far(1, 0)
-    start_far(6)
-    make_far(2, 1)
-    start_far(7)
-    make_far(3, 0)
-    make_far(3, 1)
-    start_far(8)
     own_chunk(0)
     own_chunk(1)
     own_chunk(2)
@@ -410,8 +415,7 @@
         return total[k, here, late[b]] + recv_far[k, b, here, :].astype(F32)
 
     def send_alone(side):
-        wait_far(4 + side)
-        x_send[2 + side] = late_rows(1 + side, 1 - side, pl.ds(0, rows)).astype(BF16)
+        x_send[2 + side] = total[1 + side, :, late[1 - side]].astype(BF16)
         x_alone[side].start()
 
     add_near(0)
@@ -422,27 +426,38 @@
         add_near(1 + side)
         e_send[2 + side] = total[1 + side, :, early[1 - side]].astype(BF16)
         e[1][side].start()
+    for b in range(2):
+        last_far[b] = chunk_of(r_far, 3, pl.ds(b * (PW // 2), PW // 2))
     for i, here in enumerate(halves):
         for side in range(2):
             wait_far(2 * i + side)
             x_send[side, here, :] = late_rows(0, side, here).astype(BF16)
             x_two[i][side].start()
-    send_near_chunk(3)
-    own_chunk(3)
-    send_alone(0)
+
+    @pl.when(far_ok)
+    def _():
+        for b in range(2):
+            beside_copies[1 - b].wait_recv()
+            send_far[3, b] = (last_far[b] + beside[b].astype(F32)).astype(BF16)
+
+    start_far(6)
+    for side in range(2):
+        send_alone(side)
     for side in range(2):
         e[0][side].wait_recv()
         e_send[4 + side] = (total[1 + side, :, early[side]] + e_recv[side].astype(F32)).astype(BF16)
         e[2][side].start()
-    send_alone(1)
-    add_near(3)
-    for side in range(2):
-        wait_far(6 + side)
-        for i, here in enumerate(halves):
+    send_near_chunk(3)
+    own_chunk(3)
+    for side in range(2):
+        wait_far(4 + side)
+    for i, here in enumerate(halves):
+        for side in range(2):
             x_two[i][side].wait_recv()
             came = x_recv[side, here, :].astype(F32)
             x_send[4 + side, here, :] = (late_rows(1 + side, side, here) + came).astype(BF16)
             x_sum[i][side].start()
+    add_near(3)
     for side in range(2):
         e[1][side].wait_recv()
         e[2][side].wait_recv()
@@ -450,13 +465,13 @@
         out_ref[:, early[side]] = (
             total[3, :, early[side]] + e_recv[4 + side].astype(F32) + e_recv[3 - side].astype(F32)
         )
-    wait_far(8)
+    wait_far(6)
     for side in range(2):
         x_alone[side].wait_recv()
     for side in range(2):
         total[3, :, late[side]] = late_rows(3, side, pl.ds(0, rows)) + x_recv[3 - side].astype(F32)
-    for side in range(2):
-        for i, here in enumerate(halves):
+    for i, here in enumerate(halves):
+        for side in range(2):
             x_sum[i][side].wait_recv()
             out_ref[here, late[side]] = total[3, here, late[side]] + x_recv[4 + side, here, :].astype(F32)
 
@@ -475,7 +490,7 @@
 
     @pl.when(far_ok)
     def _():
-        for copy in list(own_far.values()) + far_copies:
+        for copy in list(own_far.values()) + far_copies + beside_copies:
             copy.wait_send()
 
         @pl.when(has_r)
@@ -514,6 +529,8 @@
             pltpu.VMEM((n_cross, rows, PW), BF16),
             pltpu.VMEM((n_cross, 2, rows, PW // 2), BF16),
             pltpu.VMEM((n_cross, rows, PW), BF16),
+            pltpu.VMEM((2, rows, PW // 2), F32),
+            pltpu.VMEM((2, rows, PW // 2), BF16),
             pltpu.VMEM((n_cross, rows, CW), F32),
             pltpu.VMEM((6, rows, EARLY // 2), BF16),
             pltpu.VMEM((6, rows, EARLY // 2), BF16),

time: 35.5 us -> 35.3 us (level)
  Pallas kernels: 34.6 us -> 34 us
    pallas_call x1, Pallas kernels: 34.6 us -> 34 us  [body(): pl.pallas_call(functools.partial(kernel, n_slab, n_cross), out_shape=pltp...]
where the time goes in v5:
time: 35.3 us; the launch traced here: 34.8 us
  Pallas kernels  34 us (96%)
  local copies, waits for them, and re-layouts  0.77 us (2%)
    pallas_call x1, Pallas kernels, body(): pl.pallas_call(functools.partial(kernel, n_slab, n_cross), out_shape=pltp...  34 us
    unnamed x1, local copies, waits for them, and re-layouts  0.77 us

profile of v5, /device:TPU:56, one launch (start us, length us, event | category | flops | bytes accessed | tf_op | source)
XLA Modules:
  0.0 34.8 jit_solution(11641615055800667884)
XLA Ops:
  0.0 34.0 %shard_map.73 = f32[64,1792]{1,0:T(8,128)S(1)} custom-call(bf16[2,7,128,128]{3,2,1,0:T(8,128)(2,1)} %a_hbm.1, bf16[4,128,128]{2,1,0:T(8,128)(2,1)} %o_hbm.1, bf16[768,128]{1,0:T(8,128)(2,1)} %bitcast.1, s32[2,7]{1,0:T(2,128)} %a_cols_hbm.1, s32[4]{0:T(128)} %over_rows_hbm.1, s32[4]{0:T(128)} %over_cols_hbm.1, s32[2,3]{1,0:T(2,128)} %p_cols_hbm.1), custom_call_target="tpu_custom_call" | custom-call | tf_op jit(solution)/shard_map/pallas_call | solution.py:510
  34.1 0.8 %copy.9 = f32[64,1792]{1,0:T(8,128)} copy(f32[64,1792]{1,0:T(8,128)S(1)} %shard_map.73) | data formatting | bytes 917504

commit v6 on v5

--- a/solution.py
+++ b/solution.py
@@ -23,6 +23,8 @@
 BROWS = MARKS + NCH * TILE
 RELAYED = (0, 1, 2, 3)
 TURNED = (4, 5)
+RUN = 16
+CUTS = 4
 F32 = jnp.float32
 BF16 = jnp.bfloat16
 
@@ -30,10 +32,10 @@
     NCH * i for i in range(10)
 )
 FAR0 = 10 * NCH
-BESIDE = FAR0 + 7
+BESIDE = FAR0 + 2 * CUTS + 3
 NEAR0 = BESIDE + 2
 X0 = NEAR0 + 4
-N_SEMS = X0 + 16
+N_SEMS = X0 + 8 + 4 * CUTS
 
 
 def dot(a, b):
@@ -55,6 +57,9 @@
     near = s + 1 - 2 * core
     far = s - 1 + 2 * core
     far_ok = jnp.logical_and(far >= 0, far < n_slab)
+    begins = lax.rem(s, RUN) == 0
+    ends = lax.rem(s, RUN) == RUN - 1
+    relays_far = jnp.logical_and(far_ok, jnp.logical_not(ends))
     right = lax.rem(c + 1, n_cross)
     left = lax.rem(c + n_cross - 1, n_cross)
     has_l = c > 0
@@ -62,7 +67,7 @@
     r_near = 2 - 2 * core
     r_far = 2 * core
     rows = CB * TILE // n_cross
-    part_rows = rows // 2
+    part_rows = rows // CUTS
 
     def device(slab, cross):
         return {"slab": slab, "cross": cross}
@@ -145,8 +150,8 @@
     rel_l_far = halo_copies(3, 3 * r_near, REL_L_FAR, far, c, RELAYED)
     rel_r_near = halo_copies(5, 3 * r_far + 2, REL_R_NEAR, near, c)
     rel_r_far = halo_copies(5, 3 * r_near + 2, REL_R_FAR, far, c, RELAYED)
-    turn_r = halo_copies(3 * r_far + 1, 3 * r_far, TURN_R, s, right, TURNED)
-    turn_l = halo_copies(3 * r_far + 1, 3 * r_far + 2, TURN_L, s, left, TURNED)
+    turn_r = halo_copies(3 * r_far + 1, 3 * r_far, TURN_R, s, right)
+    turn_l = halo_copies(3 * r_far + 1, 3 * r_far + 2, TURN_L, s, left)
 
     for h in range(NCH):
 
@@ -204,7 +209,7 @@
             own_r[h].wait_recv()
             if h in RELAYED:
 
-                @pl.when(far_ok)
+                @pl.when(relays_far)
                 def _():
                     rel_l_far[h].start()
 
@@ -215,24 +220,27 @@
             own_l[h].wait_recv()
             if h in RELAYED:
 
-                @pl.when(far_ok)
+                @pl.when(relays_far)
                 def _():
                     rel_r_far[h].start()
 
             rel_r_near[h].start()
 
     def turn(h):
-        @pl.when(far_ok)
-        def _():
-            own_far[h].wait_recv()
-
-            @pl.when(has_r)
-            def _():
-                turn_r[h].start()
-
-            @pl.when(has_l)
-            def _():
-                turn_l[h].start()
+        own_far[h].wait_recv()
+
+        @pl.when(has_r)
+        def _():
+            turn_r[h].start()
+
+        @pl.when(has_l)
+        def _():
+            turn_l[h].start()
+
+    def turn_unless_late(h):
+        @pl.when(jnp.logical_and(far_ok, jnp.logical_not(begins)))
+        def _():
+            turn(h)
 
     def product_of(r, u, count, j):
         right_side = dense[pl.ds(6 * r + 2 * u, 2 * count), :, pl.ds(j * WIDTH, WIDTH)]
@@ -269,10 +277,19 @@
     def far_rows(n):
         for u, has, relayed, turned in far_sides:
 
-            @pl.when(jnp.logical_and(far_ok, has))
-            def _():
-                for h in (first, rest)[n]:
-                    (relayed if h in RELAYED else turned)[h].wait_recv()
+            for h in (first, rest)[n]:
+                comes = jnp.logical_and(far_ok, has)
+                if h in RELAYED:
+
+                    @pl.when(jnp.logical_and(comes, jnp.logical_not(begins)))
+                    def _():
+                        relayed[h].wait_recv()
+
+                    comes = jnp.logical_and(comes, begins)
+
+                @pl.when(comes)
+                def _():
+                    turned[h].wait_recv()
 
             densify(3 * r_far + u, (n,))
 
@@ -280,10 +297,10 @@
         load.wait()
     place_a(1)
     relay(0)
-    turn(TURNED[0])
+    turn_unless_late(TURNED[0])
     add_own(1)
     relay(1)
-    turn(TURNED[1])
+    turn_unless_late(TURNED[1])
     for n in range(NB):
         for q in range(3 * CB):
             block = dense[8 + n, :, pl.ds(q * TILE, TILE)]
@@ -299,13 +316,18 @@
     add_own(r_near)
     relay(4)
     near_rows(0)
-
-    @pl.when(far_ok)
+    relay(5)
+
+    @pl.when(jnp.logical_and(far_ok, begins))
+    def _():
+        for h in TURNED + RELAYED:
+            turn(h)
+
+    @pl.when(jnp.logical_and(far_ok, jnp.logical_not(begins)))
     def _():
         for h in RELAYED:
             own_far[h].wait_recv()
 
-    relay(5)
     add_own(r_far)
     densify(3, (1,))
     densify(5, (1,))
@@ -328,14 +350,14 @@
         lhs = p_turned[pl.ds(pl.multiple_of(q * WIDTH + order[k] * rows, rows), rows), :]
         return dot(lhs, prod[:, at])
 
-    halves = (pl.ds(0, part_rows), pl.ds(part_rows, part_rows))
+    halves = [pl.ds(i * part_rows, part_rows) for i in range(CUTS)]
     pieces = [(0, b, here) for here in halves for b in range(2)]
     pieces += [(k, b, pl.ds(0, rows)) for k, b in ((1, 0), (2, 1))]
     far_copies = [
         remote(send_far.at[k, b, here], recv_far.at[k, b, here], FAR0 + i, far, c)
         for i, (k, b, here) in enumerate(pieces)
     ]
-    far_copies.append(remote(send_far.at[3], recv_far.at[3], FAR0 + 6, far, c))
+    far_copies.append(remote(send_far.at[3], recv_far.at[3], FAR0 + 2 * CUTS + 2, far, c))
     beside_copies = [
         remote(send_far.at[1 + side, 1 - side], beside.at[1 - side], BESIDE + side, s, (right, left)[side])
         for side in range(2)
@@ -363,7 +385,7 @@
 
     make_far(0, 0)
     make_far(0, 1)
-    start_far(0, 1, 2, 3)
+    start_far(*range(2 * CUTS))
     for side in range(2):
         make_far(1 + side, 1 - side)
 
@@ -374,7 +396,7 @@
     send_near_chunk(0)
     for side in range(2):
         make_far(1 + side, side)
-        start_far(4 + side)
+        start_far(2 * CUTS + side)
     send_near_chunk(1)
     send_near_chunk(2)
     own_chunk(0)
@@ -408,8 +430,8 @@
 
     e = [[early_copy(step, side) for side in range(2)] for step in range(3)]
     x_two = [[late_copy(0, side, here, 2 * i) for side in range(2)] for i, here in enumerate(halves)]
-    x_alone = [late_copy(1, side, pl.ds(0, rows), 4) for side in range(2)]
-    x_sum = [[late_copy(2, side, here, 6 + 2 * i) for side in range(2)] for i, here in enumerate(halves)]
+    x_alone = [late_copy(1, side, pl.ds(0, rows), 2 * CUTS) for side in range(2)]
+    x_sum = [[late_copy(2, side, here, 2 * CUTS + 2 + 2 * i) for side in range(2)] for i, here in enumerate(halves)]
 
     def late_rows(k, b, here):
         return total[k, here, late[b]] + recv_far[k, b, here, :].astype(F32)
@@ -440,7 +462,7 @@
             beside_copies[1 - b].wait_recv()
             send_far[3, b] = (last_far[b] + beside[b].astype(F32)).astype(BF16)
 
-    start_far(6)
+    start_far(2 * CUTS + 2)
     for side in range(2):
         send_alone(side)
     for side in range(2):
@@ -450,7 +472,7 @@
     send_near_chunk(3)
     own_chunk(3)
     for side in range(2):
-        wait_far(4 + side)
+        wait_far(2 * CUTS + side)
     for i, here in enumerate(halves):
         for side in range(2):
             x_two[i][side].wait_recv()
@@ -465,7 +487,7 @@
         out_ref[:, early[side]] = (
             total[3, :, early[side]] + e_recv[4 + side].astype(F32) + e_recv[3 - side].astype(F32)
         )
-    wait_far(6)
+    wait_far(2 * CUTS + 2)
     for side in range(2):
         x_alone[side].wait_recv()
     for side in range(2):
@@ -475,7 +497,7 @@
             x_sum[i][side].wait_recv()
             out_ref[here, late[side]] = total[3, here, late[side]] + x_recv[4 + side, here, :].astype(F32)
 
-    for copy in list(own_near.values()) + near_copies + e[0] + e[1] + e[2] + x_two[0] + x_two[1] + x_alone + x_sum[0] + x_sum[1]:
+    for copy in list(own_near.values()) + near_copies + e[0] + e[1] + e[2] + sum(x_two + x_sum, x_alone):
         copy.wait_send()
 
     @pl.when(has_r)
@@ -493,15 +515,22 @@
         for copy in list(own_far.values()) + far_copies + beside_copies:
             copy.wait_send()
 
-        @pl.when(has_r)
-        def _():
-            for copy in list(rel_r_far.values()) + list(turn_r.values()):
-                copy.wait_send()
-
-        @pl.when(has_l)
-        def _():
-            for copy in list(rel_l_far.values()) + list(turn_l.values()):
-                copy.wait_send()
+        for has, relayed, turned in ((has_r, rel_r_far, turn_r), (has_l, rel_l_far, turn_l)):
+
+            @pl.when(jnp.logical_and(has, relays_far))
+            def _():
+                for h in RELAYED:
+                    relayed[h].wait_send()
+
+            @pl.when(has)
+            def _():
+                for h in TURNED:
+                    turned[h].wait_send()
+
+            @pl.when(jnp.logical_and(has, begins))
+            def _():
+                for h in RELAYED:
+                    turned[h].wait_send()
 
 
 def body(n_slab, n_cross, a_tiles, a_cols, over_tiles, over_rows, over_cols, p_tiles, p_cols):

time: 35.3 us -> 36.6 us (1.037)
  Pallas kernels: 34 us -> 35.6 us
    pallas_call x1, Pallas kernels: 34 us -> 35.6 us  [body(): pl.pallas_call(functools.partial(kernel, n_slab, n_cross), out_shape=pltp...]
where the time goes in v6:
time: 36.6 us; the launch traced here: 36.4 us
  Pallas kernels  35.6 us (97%)
  local copies, waits for them, and re-layouts  0.77 us (2%)
    pallas_call x1, Pallas kernels, body(): pl.pallas_call(functools.partial(kernel, n_slab, n_cross), out_shape=pltp...  35.6 us
    unnamed x1, local copies, waits for them, and re-layouts  0.77 us

profile of v6, /device:TPU:56, one launch (start us, length us, event | category | flops | bytes accessed | tf_op | source)
XLA Modules:
  0.0 36.4 jit_solution(15798445301319377137)
XLA Ops:
  0.0 35.6 %shard_map.73 = f32[64,1792]{1,0:T(8,128)S(1)} custom-call(bf16[2,7,128,128]{3,2,1,0:T(8,128)(2,1)} %a_hbm.1, bf16[4,128,128]{2,1,0:T(8,128)(2,1)} %o_hbm.1, bf16[768,128]{1,0:T(8,128)(2,1)} %bitcast.1, s32[2,7]{1,0:T(2,128)} %a_cols_hbm.1, s32[4]{0:T(128)} %over_rows_hbm.1, s32[4]{0:T(128)} %over_cols_hbm.1, s32[2,3]{1,0:T(2,128)} %p_cols_hbm.1), custom_call_target="tpu_custom_call" | custom-call | tf_op jit(solution)/shard_map/pallas_call | solution.py:539
  35.7 0.8 %copy.9 = f32[64,1792]{1,0:T(8,128)} copy(f32[64,1792]{1,0:T(8,128)S(1)} %shard_map.73) | data formatting | bytes 917504

commit v7 on v6

--- a/solution.py
+++ b/solution.py
@@ -23,8 +23,9 @@
 BROWS = MARKS + NCH * TILE
 RELAYED = (0, 1, 2, 3)
 TURNED = (4, 5)
+TO_ENDS = (0, 1)
 RUN = 16
-CUTS = 4
+CUTS = 2
 F32 = jnp.float32
 BF16 = jnp.bfloat16
 
@@ -49,7 +50,7 @@
     a_cols, over_rows, over_cols, p_cols,
     halo, dense, a_in, o_in, a_dense, p_turned, acc, prod,
     send_far, send_near, recv_far, recv_near, last_far, beside, total,
-    e_send, e_recv, x_send, x_recv, local_sem, send_sem, recv_sem,
+    e_send, e_recv, x_send, x_recv, far_in, local_sem, send_sem, recv_sem,
 ):
     s = lax.axis_index("slab")
     c = lax.axis_index("cross")
@@ -59,7 +60,10 @@
     far_ok = jnp.logical_and(far >= 0, far < n_slab)
     begins = lax.rem(s, RUN) == 0
     ends = lax.rem(s, RUN) == RUN - 1
-    relays_far = jnp.logical_and(far_ok, jnp.logical_not(ends))
+    inside = jnp.logical_not(jnp.logical_or(begins, ends))
+    far_inside = jnp.logical_and(far_ok, inside)
+    far_begins = jnp.logical_and(far_ok, begins)
+    far_ends = jnp.logical_and(far_ok, ends)
     right = lax.rem(c + 1, n_cross)
     left = lax.rem(c + n_cross - 1, n_cross)
     has_l = c > 0
@@ -85,7 +89,7 @@
             barrier, inc=1, device_id=device(slab, cross), device_id_type=pl.DeviceIdType.MESH
         )
 
-    @pl.when(far_ok)
+    @pl.when(jnp.logical_and(far_ok, jnp.logical_not(ends)))
     def _():
         greet(far, c)
 
@@ -133,7 +137,11 @@
         value = jnp.where(row == i, p_cols[i // KP, i % KP].astype(F32), value)
     halo[4, pl.ds(0, MARKS), :] = value.astype(BF16)
     load_p.wait()
-    pl.semaphore_wait(barrier, 3 + far_ok.astype(jnp.int32))
+    pl.semaphore_wait(barrier, 3 + jnp.logical_and(far_ok, jnp.logical_not(begins)).astype(jnp.int32))
+
+    @pl.when(far_ends)
+    def _():
+        pl.semaphore_signal(far_in, inc=1, device_id=device(far, c), device_id_type=pl.DeviceIdType.MESH)
 
     def halo_copies(b, to, first, slab, cross, chunks=range(NCH)):
         copies = {}
@@ -163,7 +171,7 @@
         def _():
             own_l[h].start()
 
-    @pl.when(far_ok)
+    @pl.when(jnp.logical_and(far_ok, jnp.logical_not(begins)))
     def _():
         for h in TURNED + RELAYED:
             own_far[h].start()
@@ -209,7 +217,7 @@
             own_r[h].wait_recv()
             if h in RELAYED:
 
-                @pl.when(relays_far)
+                @pl.when(far_inside)
                 def _():
                     rel_l_far[h].start()
 
@@ -220,7 +228,7 @@
             own_l[h].wait_recv()
             if h in RELAYED:
 
-                @pl.when(relays_far)
+                @pl.when(far_inside)
                 def _():
                     rel_r_far[h].start()
 
@@ -237,8 +245,8 @@
         def _():
             turn_l[h].start()
 
-    def turn_unless_late(h):
-        @pl.when(jnp.logical_and(far_ok, jnp.logical_not(begins)))
+    def turn_inside(h):
+        @pl.when(far_inside)
         def _():
             turn(h)
 
@@ -274,18 +282,22 @@
 
             densify(3 * r_near + u, (n,))
 
+    def turned_here(h):
+        return begins if h in TO_ENDS else jnp.logical_or(begins, ends)
+
     def far_rows(n):
         for u, has, relayed, turned in far_sides:
 
             for h in (first, rest)[n]:
                 comes = jnp.logical_and(far_ok, has)
                 if h in RELAYED:
-
-                    @pl.when(jnp.logical_and(comes, jnp.logical_not(begins)))
+                    over_slab_first = turned_here(h)
+
+                    @pl.when(jnp.logical_and(comes, jnp.logical_not(over_slab_first)))
                     def _():
                         relayed[h].wait_recv()
 
-                    comes = jnp.logical_and(comes, begins)
+                    comes = jnp.logical_and(comes, over_slab_first)
 
                 @pl.when(comes)
                 def _():
@@ -297,10 +309,10 @@
         load.wait()
     place_a(1)
     relay(0)
-    turn_unless_late(TURNED[0])
+    turn_inside(TURNED[0])
     add_own(1)
     relay(1)
-    turn_unless_late(TURNED[1])
+    turn_inside(TURNED[1])
     for n in range(NB):
         for q in range(3 * CB):
             block = dense[8 + n, :, pl.ds(q * TILE, TILE)]
@@ -318,12 +330,36 @@
     near_rows(0)
     relay(5)
 
-    @pl.when(jnp.logical_and(far_ok, begins))
-    def _():
+    beyond = [h for h in range(NCH) if h not in TO_ENDS]
+
+    @pl.when(far_begins)
+    def _():
+        pl.semaphore_wait(far_in, 1)
+        for h in beyond:
+            own_far[h].start()
+        for h in TO_ENDS:
+            own_far[h].start()
+        for h in TO_ENDS:
+
+            @pl.when(has_l)
+            def _():
+                rel_l_far[h].start()
+
+            @pl.when(has_r)
+            def _():
+                rel_r_far[h].start()
+
         for h in TURNED + RELAYED:
             turn(h)
 
-    @pl.when(jnp.logical_and(far_ok, jnp.logical_not(begins)))
+    @pl.when(far_ends)
+    def _():
+        for h in beyond:
+            turn(h)
+        for h in TO_ENDS:
+            own_far[h].wait_recv()
+
+    @pl.when(far_inside)
     def _():
         for h in RELAYED:
             own_far[h].wait_recv()
@@ -517,19 +553,20 @@
 
         for has, relayed, turned in ((has_r, rel_r_far, turn_r), (has_l, rel_l_far, turn_l)):
 
-            @pl.when(jnp.logical_and(has, relays_far))
-            def _():
-                for h in RELAYED:
-                    relayed[h].wait_send()
-
             @pl.when(has)
             def _():
                 for h in TURNED:
                     turned[h].wait_send()
 
-            @pl.when(jnp.logical_and(has, begins))
-            def _():
-                for h in RELAYED:
+            for h in RELAYED:
+                relays = inside if h not in TO_ENDS else jnp.logical_not(ends)
+
+                @pl.when(jnp.logical_and(has, relays))
+                def _():
+                    relayed[h].wait_send()
+
+                @pl.when(jnp.logical_and(has, turned_here(h)))
+                def _():
                     turned[h].wait_send()
 
 
@@ -565,6 +602,7 @@
             pltpu.VMEM((6, rows, EARLY // 2), BF16),
             pltpu.VMEM((6, rows, PW // 2), BF16),
             pltpu.VMEM((6, rows, PW // 2), BF16),
+            pltpu.SemaphoreType.REGULAR,
             pltpu.SemaphoreType.DMA((7,)),
             pltpu.SemaphoreType.DMA((N_SEMS,)),
             pltpu.SemaphoreType.DMA((N_SEMS,)),

time: 36.6 us -> 35.2 us (0.962)
  Pallas kernels: 35.6 us -> 34.2 us
    pallas_call x1, Pallas kernels: 35.6 us -> 34.2 us  [body(): pl.pallas_call(functools.partial(kernel, n_slab, n_cross), out_shape=pltp...]
where the time goes in v7:
time: 35.2 us; the launch traced here: 35 us
  Pallas kernels  34.2 us (97%)
  local copies, waits for them, and re-layouts  0.77 us (2%)
    pallas_call x1, Pallas kernels, body(): pl.pallas_call(functools.partial(kernel, n_slab, n_cross), out_shape=pltp...  34.2 us
    unnamed x1, local copies, waits for them, and re-layouts  0.77 us

profile of v7, /device:TPU:56, one launch (start us, length us, event | category | flops | bytes accessed | tf_op | source)
XLA Modules:
  0.0 35.0 jit_solution(3161112834792807529)
XLA Ops:
  0.0 34.2 %shard_map.73 = f32[64,1792]{1,0:T(8,128)S(1)} custom-call(bf16[2,7,128,128]{3,2,1,0:T(8,128)(2,1)} %a_hbm.1, bf16[4,128,128]{2,1,0:T(8,128)(2,1)} %o_hbm.1, bf16[768,128]{1,0:T(8,128)(2,1)} %bitcast.1, s32[2,7]{1,0:T(2,128)} %a_cols_hbm.1, s32[4]{0:T(128)} %over_rows_hbm.1, s32[4]{0:T(128)} %over_cols_hbm.1, s32[2,3]{1,0:T(2,128)} %p_cols_hbm.1), custom_call_target="tpu_custom_call" | custom-call | tf_op jit(solution)/shard_map/pallas_call | solution.py:576
  34.3 0.8 %copy.9 = f32[64,1792]{1,0:T(8,128)} copy(f32[64,1792]{1,0:T(8,128)S(1)} %shard_map.73) | data formatting | bytes 917504

commit v8 on v7

--- a/solution.py
+++ b/solution.py
@@ -330,41 +330,6 @@
     near_rows(0)
     relay(5)
 
-    beyond = [h for h in range(NCH) if h not in TO_ENDS]
-
-    @pl.when(far_begins)
-    def _():
-        pl.semaphore_wait(far_in, 1)
-        for h in beyond:
-            own_far[h].start()
-        for h in TO_ENDS:
-            own_far[h].start()
-        for h in TO_ENDS:
-
-            @pl.when(has_l)
-            def _():
-                rel_l_far[h].start()
-
-            @pl.when(has_r)
-            def _():
-                rel_r_far[h].start()
-
-        for h in TURNED + RELAYED:
-            turn(h)
-
-    @pl.when(far_ends)
-    def _():
-        for h in beyond:
-            turn(h)
-        for h in TO_ENDS:
-            own_far[h].wait_recv()
-
-    @pl.when(far_inside)
-    def _():
-        for h in RELAYED:
-            own_far[h].wait_recv()
-
-    add_own(r_far)
     densify(3, (1,))
     densify(5, (1,))
     add_sides(1)
@@ -374,6 +339,41 @@
         at = pl.ds(pl.multiple_of((3 - 3 * core + j) * WIDTH, WIDTH), WIDTH)
         prod[:, at] = acc[:, at].astype(BF16)
 
+    beyond = [h for h in range(NCH) if h not in TO_ENDS]
+
+    @pl.when(far_begins)
+    def _():
+        pl.semaphore_wait(far_in, 1)
+        for h in beyond:
+            own_far[h].start()
+        for h in TO_ENDS:
+            own_far[h].start()
+        for h in TO_ENDS:
+
+            @pl.when(has_l)
+            def _():
+                rel_l_far[h].start()
+
+            @pl.when(has_r)
+            def _():
+                rel_r_far[h].start()
+
+        for h in TURNED + RELAYED:
+            turn(h)
+
+    @pl.when(far_ends)
+    def _():
+        for h in beyond:
+            turn(h)
+        for h in TO_ENDS:
+            own_far[h].wait_recv()
+
+    @pl.when(far_inside)
+    def _():
+        for h in RELAYED:
+            own_far[h].wait_recv()
+
+    add_own(r_far)
     far_rows(0)
     far_rows(1)
     for j in range(3):
@@ -420,8 +420,9 @@
             total[k, :, pl.ds((j + 1) * WIDTH, WIDTH)] = chunk_of(1, k, pl.ds(j * WIDTH, WIDTH))
 
     make_far(0, 0)
+    start_far(0)
     make_far(0, 1)
-    start_far(*range(2 * CUTS))
+    start_far(*range(1, 2 * CUTS))
     for side in range(2):
         make_far(1 + side, 1 - side)
 

time: 35.2 us -> 36.6 us (1.040)
  Pallas kernels: 34.2 us -> 35.7 us
    pallas_call x1, Pallas kernels: 34.2 us -> 35.7 us  [body(): pl.pallas_call(functools.partial(kernel, n_slab, n_cross), out_shape=pltp...]
where the time goes in v8:
time: 36.6 us; the launch traced here: 36.5 us
  Pallas kernels  35.7 us (98%)
  local copies, waits for them, and re-layouts  0.77 us (2%)
    pallas_call x1, Pallas kernels, body(): pl.pallas_call(functools.partial(kernel, n_slab, n_cross), out_shape=pltp...  35.7 us
    unnamed x1, local copies, waits for them, and re-layouts  0.77 us

profile of v8, /device:TPU:56, one launch (start us, length us, event | category | flops | bytes accessed | tf_op | source)
XLA Modules:
  0.0 36.5 jit_solution(7364107328426968111)
XLA Ops:
  0.0 35.7 %shard_map.73 = f32[64,1792]{1,0:T(8,128)S(1)} custom-call(bf16[2,7,128,128]{3,2,1,0:T(8,128)(2,1)} %a_hbm.1, bf16[4,128,128]{2,1,0:T(8,128)(2,1)} %o_hbm.1, bf16[768,128]{1,0:T(8,128)(2,1)} %bitcast.1, s32[2,7]{1,0:T(2,128)} %a_cols_hbm.1, s32[4]{0:T(128)} %over_rows_hbm.1, s32[4]{0:T(128)} %over_cols_hbm.1, s32[2,3]{1,0:T(2,128)} %p_cols_hbm.1), custom_call_target="tpu_custom_call" | custom-call | tf_op jit(solution)/shard_map/pallas_call | solution.py:577
  35.7 0.8 %copy.9 = f32[64,1792]{1,0:T(8,128)} copy(f32[64,1792]{1,0:T(8,128)S(1)} %shard_map.73) | data formatting | bytes 917504

commit v9 on v7

--- a/solution.py
+++ b/solution.py
@@ -330,6 +330,9 @@
     near_rows(0)
     relay(5)
 
+    densify(3, (1,))
+    densify(5, (1,))
+    add_sides(1)
     beyond = [h for h in range(NCH) if h not in TO_ENDS]
 
     @pl.when(far_begins)
@@ -365,9 +368,6 @@
             own_far[h].wait_recv()
 
     add_own(r_far)
-    densify(3, (1,))
-    densify(5, (1,))
-    add_sides(1)
     near_rows(1)
     add_sides(r_near)
     for j in range(2):

time: 35.2 us -> 35.7 us (1.014)
  Pallas kernels: 34.2 us -> 34.8 us
    pallas_call x1, Pallas kernels: 34.2 us -> 34.8 us  [body(): pl.pallas_call(functools.partial(kernel, n_slab, n_cross), out_shape=pltp...]
where the time goes in v9:
time: 35.7 us; the launch traced here: 35.5 us
  Pallas kernels  34.8 us (97%)
  local copies, waits for them, and re-layouts  0.77 us (2%)
    pallas_call x1, Pallas kernels, body(): pl.pallas_call(functools.partial(kernel, n_slab, n_cross), out_shape=pltp...  34.8 us
    unnamed x1, local copies, waits for them, and re-layouts  0.77 us

profile of v9, /device:TPU:56, one launch (start us, length us, event | category | flops | bytes accessed | tf_op | source)
XLA Modules:
  0.0 35.5 jit_solution(3183256388251167917)
XLA Ops:
  0.0 34.8 %shard_map.73 = f32[64,1792]{1,0:T(8,128)S(1)} custom-call(bf16[2,7,128,128]{3,2,1,0:T(8,128)(2,1)} %a_hbm.1, bf16[4,128,128]{2,1,0:T(8,128)(2,1)} %o_hbm.1, bf16[768,128]{1,0:T(8,128)(2,1)} %bitcast.1, s32[2,7]{1,0:T(2,128)} %a_cols_hbm.1, s32[4]{0:T(128)} %over_rows_hbm.1, s32[4]{0:T(128)} %over_cols_hbm.1, s32[2,3]{1,0:T(2,128)} %p_cols_hbm.1), custom_call_target="tpu_custom_call" | custom-call | tf_op jit(solution)/shard_map/pallas_call | solution.py:576
  34.8 0.8 %copy.9 = f32[64,1792]{1,0:T(8,128)} copy(f32[64,1792]{1,0:T(8,128)S(1)} %shard_map.73) | data formatting | bytes 917504
